TPU v7x, 32 devices: a whole 2x2x4 slice. The times are simulated.
32 devices in a mesh: lat: 4 (over x, core), lon: 8 (over z, y).
Axes of the slice: x: 2, y: 2, z: 4, core: 2. Of those that a mesh axis runs over, the one named last changes fastest.
Arguments:
- prediction_fields: float32 [4, 69, 360, 512], P(None, None, 'lon', 'lat'), may hold values from -16 to 16
- verifying_state: float32 [69, 360, 512], P(None, 'lon', 'lat'), may hold values from -16 to 16
- normal_state: float32 [69, 360, 512], P(None, 'lon', 'lat'), may hold values from -16 to 16
- evaluated_point_flag: int32 [360, 512], P('lon', 'lat'), may hold values 0 or 1
- parallels_each_strip: int32 [4], replicated, may hold values from 1 to 128, 361 in all
Outputs:
- parallel_quadratic_error: float32 [4, 69, 512], P(None, None, 'lat')
- parallel_systematic_error: float32 [4, 69, 512], P(None, None, 'lat')
- parallel_pattern_skill: float32 [4, 69, 512], P(None, None, 'lat')
- rmse: float32 [4, 69], replicated
- systematic_error: float32 [4, 69], replicated
- pattern_skill: float32 [4, 69], replicated
Inputs may be any that keep to these rules, and one draw needn't show every extreme that they name: `parallels_each_strip`: they sum to 361, and some band holds exactly 128 rows.
All inputs are finite; a program needn't handle non-finite values.
Results may differ from a plain program's by a relative error of at most 0.00002.
Values sent between devices are 32-bit elements.
No kernel may reach another device: no remote copies, remote signals or barrier semaphores. Data moves between devices by JAX's collectives and lax.ppermute only.
A program may use at most 64 MiB of HBM per device.

v0:
```python
import functools
import math

import jax
import jax.numpy as jnp
import numpy as np
from jax import lax
from jax.experimental import pallas as pl
from jax.experimental.pallas import tpu as pltpu
from jax.sharding import PartitionSpec as P


MEAN_ROWS = 90
FLOOR = 0.1
SUB = 8
UNROLL = 9
NEAR = (1, 3, 2)
BACK = (3, 1, 2)


def up(n, m):
    return -(-n // m) * m


class Plan:
    def __init__(self, leads, nvar, nlon, width, lats, lons):
        self.leads, self.nvar, self.nlon, self.width = leads, nvar, nlon, width
        self.lats, self.lons = lats, lons
        self.lat_total = MEAN_ROWS * lats + 1
        self.lon_total = nlon * lons
        self.quad = 4
        self.groups = nvar // SUB
        self.chunks = self.groups // self.quad
        self.top = self.groups * SUB
        self.extra = nvar - self.top
        self.sums = 4 * leads + 1
        self.slots = SUB // self.quad
        self.gsum = up(self.sums, SUB)
        self.xrow = self.sums * SUB
        self.rrows = [self.xrow] * (self.chunks - 1) + [up(self.xrow + self.sums * self.slots, SUB)]
        self.prow = SUB * leads
        self.grow0 = 3 * self.prow
        self.grows = [self.grow0 + self.gsum] * (self.chunks - 1) + [self.grow0 + 3 * self.slots * leads]

    def last(self, c):
        return c == self.chunks - 1

    def fits(self):
        return (
            self.lons == 2 * self.quad
            and self.chunks == 2
            and self.groups == self.chunks * self.quad
            and self.extra > 0
            and self.leads == 4
            and self.width == 128
        )


def sums_kernel(pn, pred, truth, norm, flag, rows, *refs):
    msgs = refs[:pn.quad]
    acc, wout, vp, vt, vn, vf, sp, keep, sem = refs[pn.quad:]
    w, lv = pn.width, pn.leads
    per = pn.nlon * lv
    starts = [SUB * g for g in range(pn.groups)] + [pn.top]
    sizes = [SUB] * pn.groups + [pn.extra]
    copies = [
        pltpu.make_async_copy(rows, sp, sem.at[0]),
        pltpu.make_async_copy(flag, vf, sem.at[1]),
    ]
    for i, (v, n) in enumerate(zip(starts, sizes)):
        copies += [
            pltpu.make_async_copy(norm.at[:, pl.ds(v, n)], vn.at[:, pl.ds(v, n)], sem.at[3 * i + 2]),
            pltpu.make_async_copy(truth.at[:, pl.ds(v, n)], vt.at[:, pl.ds(v, n)], sem.at[3 * i + 3]),
            pltpu.make_async_copy(pred.at[pl.ds(v, n)], vp.at[pl.ds(v, n)], sem.at[3 * i + 4]),
        ]
    for c in copies:
        c.start()
    for j in range(pn.sums):
        acc[j, pl.ds(pn.top, SUB), :] = jnp.zeros((SUB, w), jnp.float32)
    me_lat = lax.axis_index("lat")
    quarter = lax.rem(lax.axis_index("lon"), pn.quad)
    copies[0].wait()
    first = jnp.int32(0)
    for b in range(pn.lats):
        first = first + jnp.where(b < me_lat, sp[b], 0)
    slot = lax.broadcasted_iota(jnp.int32, (SUB, w), 1)
    inside = slot < sp[me_lat]
    row = first + slot
    fold = jnp.minimum(row, pn.lat_total - 1 - row).astype(jnp.float32)
    x = fold * np.float32(math.pi / (pn.lat_total - 1))
    x2 = x * x
    poly = jnp.full_like(x, 1.0 / math.factorial(13))
    for d in (11, 9, 7, 5, 3, 1):
        poly = poly * x2 * (-1.0) + 1.0 / math.factorial(d)
    total = float(np.sum(np.sin(np.pi * np.arange(pn.lat_total) / (pn.lat_total - 1))))
    wout[...] = jnp.where(inside, poly * x * np.float32(pn.lat_total / total), 0.0)
    copies[1].wait()
    keep[...] = jnp.where(inside[0:1], vf[...], 0).astype(jnp.float32)
    flat = vp.reshape(pn.nvar * per, w)
    for i, (v, n) in enumerate(zip(starts, sizes)):
        for c in copies[3 * i + 2:3 * i + 5]:
            c.wait()
        zero = jnp.zeros((n, w), jnp.float32)

        def body(l, c, v=v, n=n):
            k = keep[pl.ds(l, n, stride=0), :]
            a = vn[l, pl.ds(v, n), :]
            t = (vt[l, pl.ds(v, n), :] - a) * k
            a = a * k
            out = []
            for q in range(lv):
                f = flat[pl.ds(v * per + l * lv + q, n, stride=per), :] * k - a
                e = f - t
                out.append((c[q] + e * e, c[lv + q] + e, c[2 * lv + q] + f * t, c[3 * lv + q] + f * f))
            return tuple(out[q][m] for m in range(4) for q in range(lv)) + (c[4 * lv] + t * t,)

        c = lax.fori_loop(0, pn.nlon, body, (zero,) * pn.sums, unroll=UNROLL)
        for j in range(pn.sums):
            acc[j, pl.ds(v, n), :] = c[j]
    for c in range(pn.chunks):
        for k in range(pn.quad):
            p = quarter ^ k
            base = pl.multiple_of(SUB * (pn.chunks * p + c), SUB)
            at = sum(pn.rrows[:c])
            for j in range(pn.sums):
                msgs[k][pl.ds(at + j * SUB, SUB), :] = acc[j, pl.ds(base, SUB), :]
            if pn.last(c):
                for j in range(pn.sums):
                    msgs[k][pl.ds(at + pn.xrow + j * pn.slots, pn.slots), :] = acc[
                        j, pl.ds(pn.top + p, pn.slots, stride=pn.quad), :
                    ]
                used = pn.xrow + pn.sums * pn.slots
                if used < pn.rrows[c]:
                    msgs[k][pl.ds(at + used, pn.rrows[c] - used), :] = jnp.zeros((pn.rrows[c] - used, w), jnp.float32)


def weigh_kernel(pn, wt, acc, gout):
    gout[...] = jnp.zeros((pn.gsum, pn.width), jnp.float32)
    for j in range(pn.sums):
        d = lax.dot_general(
            wt[...],
            acc[j],
            (((1,), (1,)), ((), ())),
            precision=lax.Precision.HIGHEST,
            preferred_element_type=jnp.float32,
        )
        gout[pl.ds(j, 1), pl.ds(0, pn.top + SUB)] = d[0:1]


def add_kernel(pn, own, r1, r2, r3, g, out):
    n = sum(pn.rrows)
    out[pl.ds(0, n), :] = (own[...] + r1[...]) + (r2[...] + r3[...])
    out[pl.ds(n, pn.gsum), :] = g[...]


def metrics(sq, off, pr, sp, tt, n):
    skill = (pr / n) / jnp.sqrt(jnp.maximum(sp / n, FLOOR) * jnp.maximum(tt / n, FLOOR))
    return sq / n, off / n, skill


def final_kernel(pn, own, far, out):
    n = np.float32(pn.lon_total)
    lv = pn.leads

    def rows(r, m):
        return own[pl.ds(r, m), :] + far[pl.ds(r, m), :]

    for c in range(pn.chunks):
        at, to = sum(pn.rrows[:c]), sum(pn.grows[:c])
        parts = [(0, SUB, 0)]
        if pn.last(c):
            parts.append((pn.xrow, pn.slots, pn.grow0))
        for x, m, y in parts:
            tt = rows(at + x + 4 * lv * m, m)
            for q in range(lv):
                vals = metrics(*(rows(at + x + (d * lv + q) * m, m) for d in range(4)), tt, n)
                for i in range(3):
                    out[pl.ds(to + y + i * m * lv + q, m, stride=lv), :] = vals[i]
    out[pl.ds(pn.grow0, pn.gsum), :] = rows(sum(pn.rrows), pn.gsum)


def place_kernel(pn, *refs):
    lv = pn.leads
    quarter = lax.rem(lax.axis_index("lon"), pn.quad)
    base = refs[:pn.quad]
    got = [[r.at[pl.ds(sum(pn.grows[:c]), pn.grows[c])] for r in base] for c in range(pn.chunks)]
    outs = refs[pn.quad:]
    flats = [outs[i].reshape(pn.nvar * lv, pn.width) for i in range(3)]
    for k in range(pn.quad):
        p = quarter ^ k
        for i in range(3):
            for c in range(pn.chunks):
                base = pl.multiple_of((pn.chunks * p + c) * pn.prow, SUB)
                flats[i][pl.ds(base, pn.prow), :] = got[c][k][pl.ds(i * pn.prow, pn.prow), :]
            for s in range(pn.slots):
                @pl.when(p + s * pn.quad < pn.extra)
                def _(i=i, s=s, k=k, p=p):
                    outs[i][pn.top + p + s * pn.quad] = got[-1][k][
                        pl.ds(pn.grow0 + (i * pn.slots + s) * lv, lv), :
                    ]
    a, b, c, d = (r[pl.ds(pn.grow0, pn.gsum), :] for r in got[0])
    g = (a + b) + (c + d)
    n = np.float32(pn.lat_total * pn.lon_total)
    mse, off, skill = metrics(*(g[m * lv:(m + 1) * lv] for m in range(4)), g[4 * lv:4 * lv + 1], n)
    outs[3][...] = jnp.sqrt(jnp.maximum(mse, FLOOR))[:, : pn.nvar]
    outs[4][...] = off[:, : pn.nvar]
    outs[5][...] = skill[:, : pn.nvar]


def fast(pn, pred, truth, norm, flag, rows):
    f32 = jnp.float32
    w, lv = pn.width, pn.leads
    vm = pl.BlockSpec(memory_space=pltpu.VMEM)
    hbm = pl.BlockSpec(memory_space=pltpu.HBM)
    pred = jnp.transpose(pred, (1, 2, 0, 3))
    truth = jnp.transpose(truth, (1, 0, 2))
    norm = jnp.transpose(norm, (1, 0, 2))
    large = pltpu.CompilerParams(vmem_limit_bytes=24 * 2**20)
    small = pltpu.CompilerParams(vmem_limit_bytes=8 * 2**20)

    def arr(*shape):
        return jax.ShapeDtypeStruct(shape, f32)

    def call(kernel, out, *args):
        return pl.pallas_call(
            kernel,
            out_shape=out,
            in_specs=[vm] * len(args),
            out_specs=jax.tree.map(lambda _: vm, out),
            compiler_params=small,
        )(*args)

    def swap(x, k):
        return lax.ppermute(x, "lon", [(i, i ^ k) for i in range(pn.lons)])

    inputs = [pltpu.with_memory_space_constraint(a, pltpu.HBM) for a in (pred, truth, norm, flag, rows)]
    *msgs, acc, wt = pl.pallas_call(
        functools.partial(sums_kernel, pn),
        out_shape=[arr(sum(pn.rrows), w)] * pn.quad
        + [arr(pn.sums, pn.top + SUB, w), arr(SUB, w)],
        in_specs=[hbm] * 5,
        out_specs=[vm] * (pn.quad + 2),
        scratch_shapes=[
            pltpu.VMEM(pred.shape, f32),
            pltpu.VMEM(truth.shape, f32),
            pltpu.VMEM(norm.shape, f32),
            pltpu.VMEM(flag.shape, jnp.int32),
            pltpu.SMEM(rows.shape, jnp.int32),
            pltpu.VMEM(flag.shape, f32),
            pltpu.SemaphoreType.DMA((2 + 3 * (pn.groups + 1),)),
        ],
        compiler_params=large,
        name="sums",
    )(*inputs)
    near = {k: swap(msgs[k], k) for k in NEAR}
    g = call(functools.partial(weigh_kernel, pn), arr(pn.gsum, w), wt, acc)
    step = 1
    while step < pn.lats:
        g = g + lax.ppermute(g, "lat", [(i, i ^ step) for i in range(pn.lats)])
        step *= 2
    part = call(
        functools.partial(add_kernel, pn), arr(sum(pn.rrows) + pn.gsum, w),
        msgs[0], near[1], near[2], near[3], g,
    )
    far = swap(part, pn.quad)
    done = call(functools.partial(final_kernel, pn), arr(sum(pn.grows), w), part, far)
    there = {k: swap(done, k) for k in BACK}
    got = [done, there[1], there[2], there[3]]
    outs = pl.pallas_call(
        functools.partial(place_kernel, pn),
        out_shape=[arr(pn.nvar, lv, w)] * 3 + [arr(lv, pn.nvar)] * 3,
        in_specs=[vm] * len(got),
        compiler_params=small,
        name="place",
    )(*got)
    return tuple(jnp.transpose(o, (1, 0, 2)) for o in outs[:3]) + tuple(outs[3:])


def plain(pn, pred, truth, norm, flag, rows):
    band = lax.axis_index("lat")
    ids = jnp.arange(pn.lats, dtype=jnp.int32)
    first = jnp.sum(jnp.where(ids < band, rows, 0))
    count = jnp.sum(jnp.where(ids == band, rows, 0))
    slot = jnp.arange(pn.width, dtype=jnp.int32)
    inside = slot < count
    angles = jnp.pi * jnp.arange(pn.lat_total, dtype=jnp.float32) / (pn.lat_total - 1)
    angle = jnp.pi * (first + slot).astype(jnp.float32) / (pn.lat_total - 1)
    weight = jnp.where(inside, jnp.sin(angle) * pn.lat_total / jnp.sum(jnp.sin(angles)), 0.0)
    keep = flag.astype(jnp.float32) * inside.astype(jnp.float32)[None, :]
    t = truth - norm
    f = pred - norm[None]
    e = f - t[None]
    k = keep[None, None]
    sums = jnp.concatenate(
        [
            jnp.sum(k * e * e, axis=2),
            jnp.sum(k * e, axis=2),
            jnp.sum(k * f * t[None], axis=2),
            jnp.sum(k * f * f, axis=2),
            jnp.sum(k * t[None] * t[None], axis=2),
        ],
        axis=0,
    )
    grand = lax.psum(jnp.sum(sums * weight, axis=2), ("lat", "lon"))
    zonal = lax.psum(sums, "lon")

    def finish(s, n):
        parts = [s[m * pn.leads:(m + 1) * pn.leads] for m in range(4)]
        return metrics(*parts, s[4 * pn.leads:], n)

    mse, off, skill = finish(zonal, float(pn.lon_total))
    gm, go, gs = finish(grand, float(pn.lat_total * pn.lon_total))
    return mse, off, skill, jnp.sqrt(jnp.maximum(gm, FLOOR)), go, gs


def local(pred, truth, norm, flag, rows):
    leads, nvar, nlon, width = pred.shape
    pn = Plan(leads, nvar, nlon, width, lax.axis_size("lat"), lax.axis_size("lon"))
    return (fast if pn.fits() else plain)(pn, pred, truth, norm, flag, rows)


def solution(mesh):
    in_specs = (
        P(None, None, "lon", "lat"),
        P(None, "lon", "lat"),
        P(None, "lon", "lat"),
        P("lon", "lat"),
        P(),
    )
    out_specs = (P(None, None, "lat"), P(None, None, "lat"), P(None, None, "lat"), P(), P(), P())
    return jax.shard_map(local, mesh=mesh, in_specs=in_specs, out_specs=out_specs, check_vma=False)
```

profile of v0, /device:TPU:0, one launch (start us, length us, event | category | flops | bytes accessed | tf_op | source)
XLA Modules:
  0.0 36.1 jit_solution(13290258490152449093)
XLA Ops:
  0.6 4.6 %sums.1 = (f32[312,128]{1,0:T(8,128)S(1)}, f32[312,128]{1,0:T(8,128)S(1)}, f32[312,128]{1,0:T(8,128)S(1)}, f32[312,128]{1,0:T(8,128)S(1)}, f32[17,72,128]{2,1,0:T(8,128)S(1)}, /*index=5*/f32[8,128]{1,0:T(8,128)S(1)}) custom-call(f32[69,45,4,128]{3,2,1,0:T(4,128)} %bitcast.6, f32[45,69,128]{2,1,0:T(8,128)} %bitcast.7, f32[45,69,128]{2,1,0:T(8,128)} %bitcast.8, ...), custom_call_target="tpu_custom_call" | custom-call | tf_op jit(solution)/shard_map/sums/pallas_call | solution.py:237
  5.2 3.1 %collective-permute-start = (f32[312,128]{1,0:T(8,128)S(1)}, f32[312,128]{1,0:T(8,128)S(1)}, u32[]{:S(2)}, u32[]{:S(2)}) collective-permute-start(f32[312,128]{1,0:T(8,128)S(1)} %get-tuple-element.19), channel_id=1, source_target_pairs={{0,1},{1,0},{2,3},{3,2},{4,5},{5,4},{6,7},{7,6},{8,9},{9,8},{10,11... | collective-permute-start | bytes 479240 | tf_op jit(solution)/shard_map/ppermute | solution.py:234
  8.3 1.6 %collective-permute-start.1 = (f32[312,128]{1,0:T(8,128)S(1)}, f32[312,128]{1,0:T(8,128)S(1)}, u32[]{:S(2)}, u32[]{:S(2)}) collective-permute-start(f32[312,128]{1,0:T(8,128)S(1)} %get-tuple-element.20), channel_id=1, source_target_pairs={{0,2},{1,3},{2,0},{3,1},{4,6},{5,7},{6,4},{7,5},{8,10},{9,11},{10,... | collective-permute-start | bytes 479240 | tf_op jit(solution)/shard_map/ppermute | solution.py:234
  9.9 0.0 collective-permute-start.2
  9.9 1.1 %shard_map.100 = f32[24,128]{1,0:T(8,128)S(1)} custom-call(f32[8,128]{1,0:T(8,128)S(1)} %get-tuple-element.22.wt, f32[17,72,128]{2,1,0:T(8,128)S(1)} %get-tuple-element.23.acc), custom_call_target="tpu_custom_call" | custom-call | tf_op jit(solution)/shard_map/pallas_call | solution.py:225
  10.9 0.0 collective-permute-start.3
  10.9 1.2 %collective-permute-done.3 = f32[24,128]{1,0:T(8,128)S(1)} collective-permute-done((f32[24,128]{1,0:T(8,128)S(1)}, f32[24,128]{1,0:T(8,128)S(1)}, u32[]{:S(2)}, u32[]{:S(2)}) %collective-permute-start.3) | collective-permute-done | bytes 12320 | tf_op jit(solution)/shard_map/ppermute | solution.py:259
  12.1 1.9 %collective-permute-start.4 = (f32[24,128]{1,0:T(8,128)S(1)}, f32[24,128]{1,0:T(8,128)S(1)}, u32[]{:S(2)}, u32[]{:S(2)}) collective-permute-start(f32[24,128]{1,0:T(8,128)S(1)} %add.6), channel_id=1, source_target_pairs={{0,16},{8,24},{16,0},{24,8},{1,17},{9,25},{17,1},{25,9},{2,18},{10... | collective-permute-start | bytes 36872 | tf_op jit(solution)/shard_map/ppermute | solution.py:259
  14.0 1.8 %collective-permute-done.4 = f32[24,128]{1,0:T(8,128)S(1)} collective-permute-done((f32[24,128]{1,0:T(8,128)S(1)}, f32[24,128]{1,0:T(8,128)S(1)}, u32[]{:S(2)}, u32[]{:S(2)}) %collective-permute-start.4) | collective-permute-done | bytes 12320 | tf_op jit(solution)/shard_map/ppermute | solution.py:259
  15.8 0.0 collective-permute-done.r1
  15.8 0.0 collective-permute-done.1.r2
  15.8 1.2 %collective-permute-done.2.r3 = f32[312,128]{1,0:T(8,128)S(1)} collective-permute-done((f32[312,128]{1,0:T(8,128)S(1)}, f32[312,128]{1,0:T(8,128)S(1)}, u32[]{:S(2)}, u32[]{:S(2)}) %collective-permute-start.2) | collective-permute-done | bytes 159776 | tf_op jit(solution)/shard_map/ppermute | solution.py:234
  17.1 2.8 %collective-permute-start.5 = (f32[336,128]{1,0:T(8,128)S(1)}, f32[336,128]{1,0:T(8,128)S(1)}, u32[]{:S(2)}, u32[]{:S(2)}) collective-permute-start(f32[336,128]{1,0:T(8,128)S(1)} %shard_map.101.own), channel_id=1, source_target_pairs={{0,4},{1,5},{2,6},{3,7},{4,0},{5,1},{6,2},{7,3},{8,12},{9,13},{10,... | collective-permute-start | bytes 516104 | tf_op jit(solution)/shard_map/ppermute | solution.py:234
  19.9 7.2 %collective-permute-done.5.far = f32[336,128]{1,0:T(8,128)S(1)} collective-permute-done((f32[336,128]{1,0:T(8,128)S(1)}, f32[336,128]{1,0:T(8,128)S(1)}, u32[]{:S(2)}, u32[]{:S(2)}) %collective-permute-start.5) | collective-permute-done | bytes 172064 | tf_op jit(solution)/shard_map/ppermute | solution.py:234
  27.1 0.1 shard_map.102.refs_0_
  27.2 1.5 %collective-permute-start.8 = (f32[240,128]{1,0:T(8,128)S(1)}, f32[240,128]{1,0:T(8,128)S(1)}, u32[]{:S(2)}, u32[]{:S(2)}) collective-permute-start(f32[240,128]{1,0:T(8,128)S(1)} %shard_map.102.refs_0_), channel_id=1, source_target_pairs={{0,3},{1,2},{2,1},{3,0},{4,7},{5,6},{6,5},{7,4},{8,11},{9,10},{10,... | collective-permute-start | bytes 368648 | tf_op jit(solution)/shard_map/ppermute | solution.py:234
  28.6 1.4 %collective-permute-start.7 = (f32[240,128]{1,0:T(8,128)S(1)}, f32[240,128]{1,0:T(8,128)S(1)}, u32[]{:S(2)}, u32[]{:S(2)}) collective-permute-start(f32[240,128]{1,0:T(8,128)S(1)} %shard_map.102.refs_0_), channel_id=1, source_target_pairs={{0,2},{1,3},{2,0},{3,1},{4,6},{5,7},{6,4},{7,5},{8,10},{9,11},{10,... | collective-permute-start | bytes 368648 | tf_op jit(solution)/shard_map/ppermute | solution.py:234
  30.0 0.7 %collective-permute-start.6 = (f32[240,128]{1,0:T(8,128)S(1)}, f32[240,128]{1,0:T(8,128)S(1)}, u32[]{:S(2)}, u32[]{:S(2)}) collective-permute-start(f32[240,128]{1,0:T(8,128)S(1)} %shard_map.102.refs_0_), channel_id=1, source_target_pairs={{0,1},{1,0},{2,3},{3,2},{4,5},{5,4},{6,7},{7,6},{8,9},{9,8},{10,11... | collective-permute-start | bytes 368648 | tf_op jit(solution)/shard_map/ppermute | solution.py:234
  30.7 3.2 %collective-permute-done.8.refs_3_ = f32[240,128]{1,0:T(8,128)S(1)} collective-permute-done((f32[240,128]{1,0:T(8,128)S(1)}, f32[240,128]{1,0:T(8,128)S(1)}, u32[]{:S(2)}, u32[]{:S(2)}) %collective-permute-start.8) | collective-permute-done | bytes 122912 | tf_op jit(solution)/shard_map/ppermute | solution.py:234
  33.9 0.9 %collective-permute-done.7.refs_2_ = f32[240,128]{1,0:T(8,128)S(1)} collective-permute-done((f32[240,128]{1,0:T(8,128)S(1)}, f32[240,128]{1,0:T(8,128)S(1)}, u32[]{:S(2)}, u32[]{:S(2)}) %collective-permute-start.7) | collective-permute-done | bytes 122912 | tf_op jit(solution)/shard_map/ppermute | solution.py:234
  34.8 0.4 %collective-permute-done.6.refs_1_ = f32[240,128]{1,0:T(8,128)S(1)} collective-permute-done((f32[240,128]{1,0:T(8,128)S(1)}, f32[240,128]{1,0:T(8,128)S(1)}, u32[]{:S(2)}, u32[]{:S(2)}) %collective-permute-start.6) | collective-permute-done | bytes 122912 | tf_op jit(solution)/shard_map/ppermute | solution.py:234
  35.3 0.8 %place.1 = (f32[69,4,128]{2,1,0:T(4,128)}, f32[69,4,128]{2,1,0:T(4,128)}, f32[69,4,128]{2,1,0:T(4,128)}, f32[4,69]{1,0:T(4,128)}, f32[4,69]{1,0:T(4,128)}, /*index=5*/f32[4,69]{1,0:T(4,128)}) custom-call(f32[240,128]{1,0:T(8,128)S(1)} %shard_map.102.refs_0_, f32[240,128]{1,0:T(8,128)S(1)} %collective-permute-done.6.refs_1_, ...), custom_call_target="tpu_custom_call" | custom-call | tf_op jit(solution)/shard_map/place/pallas_call | solution.py:269
  (3 shorter events, 0.0 us)
Async XLA Ops:
  5.2 10.6 %collective-permute-start = (f32[312,128]{1,0:T(8,128)S(1)}, f32[312,128]{1,0:T(8,128)S(1)}, u32[]{:S(2)}, u32[]{:S(2)}) collective-permute-start(f32[312,128]{1,0:T(8,128)S(1)} %get-tuple-element.19), channel_id=1, source_target_pairs={{0,1},{1,0},{2,3},{3,2},{4,5},{5,4},{6,7},{7,6},{8,9},{9,8},{10,11... | collective-permute-start | bytes 479240 | tf_op jit(solution)/shard_map/ppermute | solution.py:234
  8.3 7.6 %collective-permute-start.1 = (f32[312,128]{1,0:T(8,128)S(1)}, f32[312,128]{1,0:T(8,128)S(1)}, u32[]{:S(2)}, u32[]{:S(2)}) collective-permute-start(f32[312,128]{1,0:T(8,128)S(1)} %get-tuple-element.20), channel_id=1, source_target_pairs={{0,2},{1,3},{2,0},{3,1},{4,6},{5,7},{6,4},{7,5},{8,10},{9,11},{10,... | collective-permute-start | bytes 479240 | tf_op jit(solution)/shard_map/ppermute | solution.py:234
  9.9 7.2 %collective-permute-start.2 = (f32[312,128]{1,0:T(8,128)S(1)}, f32[312,128]{1,0:T(8,128)S(1)}, u32[]{:S(2)}, u32[]{:S(2)}) collective-permute-start(f32[312,128]{1,0:T(8,128)S(1)} %get-tuple-element.21), channel_id=1, source_target_pairs={{0,3},{1,2},{2,1},{3,0},{4,7},{5,6},{6,5},{7,4},{8,11},{9,10},{10,... | collective-permute-start | bytes 479240 | tf_op jit(solution)/shard_map/ppermute | solution.py:234
  10.9 1.2 %collective-permute-start.3 = (f32[24,128]{1,0:T(8,128)S(1)}, f32[24,128]{1,0:T(8,128)S(1)}, u32[]{:S(2)}, u32[]{:S(2)}) collective-permute-start(f32[24,128]{1,0:T(8,128)S(1)} %shard_map.100), channel_id=1, source_target_pairs={{0,8},{8,0},{16,24},{24,16},{1,9},{9,1},{17,25},{25,17},{2,10},{10... | collective-permute-start | bytes 36872 | tf_op jit(solution)/shard_map/ppermute | solution.py:259
  12.1 3.7 %collective-permute-start.4 = (f32[24,128]{1,0:T(8,128)S(1)}, f32[24,128]{1,0:T(8,128)S(1)}, u32[]{:S(2)}, u32[]{:S(2)}) collective-permute-start(f32[24,128]{1,0:T(8,128)S(1)} %add.6), channel_id=1, source_target_pairs={{0,16},{8,24},{16,0},{24,8},{1,17},{9,25},{17,1},{25,9},{2,18},{10... | collective-permute-start | bytes 36872 | tf_op jit(solution)/shard_map/ppermute | solution.py:259
  17.1 10.0 %collective-permute-start.5 = (f32[336,128]{1,0:T(8,128)S(1)}, f32[336,128]{1,0:T(8,128)S(1)}, u32[]{:S(2)}, u32[]{:S(2)}) collective-permute-start(f32[336,128]{1,0:T(8,128)S(1)} %shard_map.101.own), channel_id=1, source_target_pairs={{0,4},{1,5},{2,6},{3,7},{4,0},{5,1},{6,2},{7,3},{8,12},{9,13},{10,... | collective-permute-start | bytes 516104 | tf_op jit(solution)/shard_map/ppermute | solution.py:234
  27.2 6.8 %collective-permute-start.8 = (f32[240,128]{1,0:T(8,128)S(1)}, f32[240,128]{1,0:T(8,128)S(1)}, u32[]{:S(2)}, u32[]{:S(2)}) collective-permute-start(f32[240,128]{1,0:T(8,128)S(1)} %shard_map.102.refs_0_), channel_id=1, source_target_pairs={{0,3},{1,2},{2,1},{3,0},{4,7},{5,6},{6,5},{7,4},{8,11},{9,10},{10,... | collective-permute-start | bytes 368648 | tf_op jit(solution)/shard_map/ppermute | solution.py:234
  28.6 6.2 %collective-permute-start.7 = (f32[240,128]{1,0:T(8,128)S(1)}, f32[240,128]{1,0:T(8,128)S(1)}, u32[]{:S(2)}, u32[]{:S(2)}) collective-permute-start(f32[240,128]{1,0:T(8,128)S(1)} %shard_map.102.refs_0_), channel_id=1, source_target_pairs={{0,2},{1,3},{2,0},{3,1},{4,6},{5,7},{6,4},{7,5},{8,10},{9,11},{10,... | collective-permute-start | bytes 368648 | tf_op jit(solution)/shard_map/ppermute | solution.py:234
  30.0 5.3 %collective-permute-start.6 = (f32[240,128]{1,0:T(8,128)S(1)}, f32[240,128]{1,0:T(8,128)S(1)}, u32[]{:S(2)}, u32[]{:S(2)}) collective-permute-start(f32[240,128]{1,0:T(8,128)S(1)} %shard_map.102.refs_0_), channel_id=1, source_target_pairs={{0,1},{1,0},{2,3},{3,2},{4,5},{5,4},{6,7},{7,6},{8,9},{9,8},{10,11... | collective-permute-start | bytes 368648 | tf_op jit(solution)/shard_map/ppermute | solution.py:234
where the time goes:
time: 36.3 us; the launch traced here: 36.1 us
  waiting for transfers between devices  16 us (44%)
  starting transfers between devices  12.9 us (36%)
  Pallas kernels  6.58 us (18%)
  between operations  0.66 us (2%)
    ppermute x7, waiting for transfers between devices, swap(): return lax.ppermute(x, 'lon', [(i, i ^ k) for i in range(pn.lons)])  13 us
    ppermute x7, starting transfers between devices, swap(): return lax.ppermute(x, 'lon', [(i, i ^ k) for i in range(pn.lons)])  11 us
    pallas_call x1, Pallas kernels, fast(): pl.pallas_call(functools.partial(sums_kernel, pn), out_shape=[arr(sum(pn....  4.58 us
    ppermute x2, waiting for transfers between devices, fast(): g = g + lax.ppermute(g, 'lat', [(i, i ^ step) for i in range(pn.lats)])  3.01 us
    ppermute x2, starting transfers between devices, fast(): g = g + lax.ppermute(g, 'lat', [(i, i ^ step) for i in range(pn.lats)])  1.88 us
    pallas_call x3, Pallas kernels, call(): pl.pallas_call(kernel, out_shape=out, in_specs=[vm] * len(args), out_spec...  1.15 us
    pallas_call x1, Pallas kernels, fast(): pl.pallas_call(functools.partial(place_kernel, pn), out_shape=[arr(pn.nva...  0.84 us
  transfers between devices with their start and end apart: 9, of which 7 were waited for; matrix products, arithmetic and copies ran while one was open for 0% of the time, Pallas kernels for 3%

commit v1 on v0

--- a/solution.py
+++ b/solution.py
@@ -14,12 +14,9 @@
 FLOOR = 0.1
 SUB = 8
 UNROLL = 9
+PIECES = 3
 NEAR = (1, 3, 2)
 BACK = (3, 1, 2)
-
-
-def up(n, m):
-    return -(-n // m) * m
 
 
 class Plan:
@@ -34,16 +31,11 @@
         self.top = self.groups * SUB
         self.extra = nvar - self.top
         self.sums = 4 * leads + 1
-        self.slots = SUB // self.quad
-        self.gsum = up(self.sums, SUB)
         self.xrow = self.sums * SUB
-        self.rrows = [self.xrow] * (self.chunks - 1) + [up(self.xrow + self.sums * self.slots, SUB)]
+        self.rrows = self.chunks * self.xrow + 5 * self.extra
         self.prow = SUB * leads
-        self.grow0 = 3 * self.prow
-        self.grows = [self.grow0 + self.gsum] * (self.chunks - 1) + [self.grow0 + 3 * self.slots * leads]
-
-    def last(self, c):
-        return c == self.chunks - 1
+        self.grow0 = self.chunks * 3 * self.prow
+        self.grow1 = self.grow0 + 3 * self.extra
 
     def fits(self):
         return (
@@ -51,7 +43,7 @@
             and self.chunks == 2
             and self.groups == self.chunks * self.quad
             and self.extra > 0
-            and self.leads == 4
+            and self.leads == self.quad
             and self.width == 128
         )
 
@@ -61,17 +53,20 @@
     acc, wout, vp, vt, vn, vf, sp, keep, sem = refs[pn.quad:]
     w, lv = pn.width, pn.leads
     per = pn.nlon * lv
-    starts = [SUB * g for g in range(pn.groups)] + [pn.top]
-    sizes = [SUB] * pn.groups + [pn.extra]
+    groups = [(pn.top, pn.extra)] + [(SUB * g, SUB) for g in range(pn.groups)]
+    cuts = [pn.nlon * i // PIECES for i in range(PIECES + 1)]
+    pieces = [(v, n, 0, pn.nlon) for v, n in groups[:-1]]
+    pieces += [groups[-1] + (lo, hi) for lo, hi in zip(cuts, cuts[1:])]
     copies = [
         pltpu.make_async_copy(rows, sp, sem.at[0]),
         pltpu.make_async_copy(flag, vf, sem.at[1]),
     ]
-    for i, (v, n) in enumerate(zip(starts, sizes)):
+    for i, (v, n, lo, hi) in enumerate(pieces):
+        var, lon = pl.ds(v, n), pl.ds(lo, hi - lo)
         copies += [
-            pltpu.make_async_copy(norm.at[:, pl.ds(v, n)], vn.at[:, pl.ds(v, n)], sem.at[3 * i + 2]),
-            pltpu.make_async_copy(truth.at[:, pl.ds(v, n)], vt.at[:, pl.ds(v, n)], sem.at[3 * i + 3]),
-            pltpu.make_async_copy(pred.at[pl.ds(v, n)], vp.at[pl.ds(v, n)], sem.at[3 * i + 4]),
+            pltpu.make_async_copy(norm.at[lon, var], vn.at[lon, var], sem.at[3 * i + 2]),
+            pltpu.make_async_copy(truth.at[lon, var], vt.at[lon, var], sem.at[3 * i + 3]),
+            pltpu.make_async_copy(pred.at[var, lon], vp.at[var, lon], sem.at[3 * i + 4]),
         ]
     for c in copies:
         c.start()
@@ -92,15 +87,14 @@
     poly = jnp.full_like(x, 1.0 / math.factorial(13))
     for d in (11, 9, 7, 5, 3, 1):
         poly = poly * x2 * (-1.0) + 1.0 / math.factorial(d)
-    total = float(np.sum(np.sin(np.pi * np.arange(pn.lat_total) / (pn.lat_total - 1))))
-    wout[...] = jnp.where(inside, poly * x * np.float32(pn.lat_total / total), 0.0)
+    norms = float(np.sum(np.sin(np.pi * np.arange(pn.lat_total) / (pn.lat_total - 1))))
+    wout[...] = jnp.where(inside, poly * x * np.float32(pn.lat_total / norms), 0.0)
     copies[1].wait()
     keep[...] = jnp.where(inside[0:1], vf[...], 0).astype(jnp.float32)
     flat = vp.reshape(pn.nvar * per, w)
-    for i, (v, n) in enumerate(zip(starts, sizes)):
+    for i, (v, n, lo, hi) in enumerate(pieces):
         for c in copies[3 * i + 2:3 * i + 5]:
             c.wait()
-        zero = jnp.zeros((n, w), jnp.float32)
 
         def body(l, c, v=v, n=n):
             k = keep[pl.ds(l, n, stride=0), :]
@@ -114,28 +108,27 @@
                 out.append((c[q] + e * e, c[lv + q] + e, c[2 * lv + q] + f * t, c[3 * lv + q] + f * f))
             return tuple(out[q][m] for m in range(4) for q in range(lv)) + (c[4 * lv] + t * t,)
 
-        c = lax.fori_loop(0, pn.nlon, body, (zero,) * pn.sums, unroll=UNROLL)
-        for j in range(pn.sums):
-            acc[j, pl.ds(v, n), :] = c[j]
+        if lo == 0:
+            total = (jnp.zeros((n, w), jnp.float32),) * pn.sums
+        total = lax.fori_loop(lo, hi, body, total, unroll=UNROLL if hi - lo == pn.nlon else hi - lo)
+        if hi == pn.nlon:
+            for j in range(pn.sums):
+                acc[j, pl.ds(v, n), :] = total[j]
     for c in range(pn.chunks):
         for k in range(pn.quad):
             p = quarter ^ k
             base = pl.multiple_of(SUB * (pn.chunks * p + c), SUB)
-            at = sum(pn.rrows[:c])
             for j in range(pn.sums):
-                msgs[k][pl.ds(at + j * SUB, SUB), :] = acc[j, pl.ds(base, SUB), :]
-            if pn.last(c):
-                for j in range(pn.sums):
-                    msgs[k][pl.ds(at + pn.xrow + j * pn.slots, pn.slots), :] = acc[
-                        j, pl.ds(pn.top + p, pn.slots, stride=pn.quad), :
-                    ]
-                used = pn.xrow + pn.sums * pn.slots
-                if used < pn.rrows[c]:
-                    msgs[k][pl.ds(at + used, pn.rrows[c] - used), :] = jnp.zeros((pn.rrows[c] - used, w), jnp.float32)
+                msgs[k][pl.ds(c * pn.xrow + j * SUB, SUB), :] = acc[j, pl.ds(base, SUB), :]
+    for k in range(pn.quad):
+        p = quarter ^ k
+        for m in range(5):
+            j = m * lv + (p if m < 4 else 0)
+            msgs[k][pl.ds(pn.chunks * pn.xrow + m * pn.extra, pn.extra), :] = acc[j, pl.ds(pn.top, pn.extra), :]
 
 
 def weigh_kernel(pn, wt, acc, gout):
-    gout[...] = jnp.zeros((pn.gsum, pn.width), jnp.float32)
+    gout[...] = jnp.zeros((pn.sums, pn.width), jnp.float32)
     for j in range(pn.sums):
         d = lax.dot_general(
             wt[...],
@@ -148,9 +141,8 @@
 
 
 def add_kernel(pn, own, r1, r2, r3, g, out):
-    n = sum(pn.rrows)
-    out[pl.ds(0, n), :] = (own[...] + r1[...]) + (r2[...] + r3[...])
-    out[pl.ds(n, pn.gsum), :] = g[...]
+    out[pl.ds(0, pn.rrows), :] = (own[...] + r1[...]) + (r2[...] + r3[...])
+    out[pl.ds(pn.rrows, pn.sums), :] = g[...]
 
 
 def metrics(sq, off, pr, sp, tt, n):
@@ -166,39 +158,34 @@
         return own[pl.ds(r, m), :] + far[pl.ds(r, m), :]
 
     for c in range(pn.chunks):
-        at, to = sum(pn.rrows[:c]), sum(pn.grows[:c])
-        parts = [(0, SUB, 0)]
-        if pn.last(c):
-            parts.append((pn.xrow, pn.slots, pn.grow0))
-        for x, m, y in parts:
-            tt = rows(at + x + 4 * lv * m, m)
-            for q in range(lv):
-                vals = metrics(*(rows(at + x + (d * lv + q) * m, m) for d in range(4)), tt, n)
-                for i in range(3):
-                    out[pl.ds(to + y + i * m * lv + q, m, stride=lv), :] = vals[i]
-    out[pl.ds(pn.grow0, pn.gsum), :] = rows(sum(pn.rrows), pn.gsum)
+        at, to = c * pn.xrow, c * 3 * pn.prow
+        tt = rows(at + 4 * lv * SUB, SUB)
+        for q in range(lv):
+            vals = metrics(*(rows(at + (d * lv + q) * SUB, SUB) for d in range(4)), tt, n)
+            for i in range(3):
+                out[pl.ds(to + i * pn.prow + q, SUB, stride=lv), :] = vals[i]
+    x = pn.chunks * pn.xrow
+    vals = metrics(*(rows(x + m * pn.extra, pn.extra) for m in range(5)), n)
+    for i in range(3):
+        out[pl.ds(pn.grow0 + i * pn.extra, pn.extra), :] = vals[i]
+    out[pl.ds(pn.grow1, pn.sums), :] = rows(pn.rrows, pn.sums)
 
 
 def place_kernel(pn, *refs):
     lv = pn.leads
     quarter = lax.rem(lax.axis_index("lon"), pn.quad)
-    base = refs[:pn.quad]
-    got = [[r.at[pl.ds(sum(pn.grows[:c]), pn.grows[c])] for r in base] for c in range(pn.chunks)]
-    outs = refs[pn.quad:]
+    got, outs = refs[:pn.quad], refs[pn.quad:]
     flats = [outs[i].reshape(pn.nvar * lv, pn.width) for i in range(3)]
     for k in range(pn.quad):
         p = quarter ^ k
         for i in range(3):
             for c in range(pn.chunks):
                 base = pl.multiple_of((pn.chunks * p + c) * pn.prow, SUB)
-                flats[i][pl.ds(base, pn.prow), :] = got[c][k][pl.ds(i * pn.prow, pn.prow), :]
-            for s in range(pn.slots):
-                @pl.when(p + s * pn.quad < pn.extra)
-                def _(i=i, s=s, k=k, p=p):
-                    outs[i][pn.top + p + s * pn.quad] = got[-1][k][
-                        pl.ds(pn.grow0 + (i * pn.slots + s) * lv, lv), :
-                    ]
-    a, b, c, d = (r[pl.ds(pn.grow0, pn.gsum), :] for r in got[0])
+                flats[i][pl.ds(base, pn.prow), :] = got[k][pl.ds((3 * c + i) * pn.prow, pn.prow), :]
+            flats[i][pl.ds(pn.top * lv + p, pn.extra, stride=lv), :] = got[k][
+                pl.ds(pn.grow0 + i * pn.extra, pn.extra), :
+            ]
+    a, b, c, d = (r[pl.ds(pn.grow1, pn.sums), :] for r in got)
     g = (a + b) + (c + d)
     n = np.float32(pn.lat_total * pn.lon_total)
     mse, off, skill = metrics(*(g[m * lv:(m + 1) * lv] for m in range(4)), g[4 * lv:4 * lv + 1], n)
@@ -236,7 +223,7 @@
     inputs = [pltpu.with_memory_space_constraint(a, pltpu.HBM) for a in (pred, truth, norm, flag, rows)]
     *msgs, acc, wt = pl.pallas_call(
         functools.partial(sums_kernel, pn),
-        out_shape=[arr(sum(pn.rrows), w)] * pn.quad
+        out_shape=[arr(pn.rrows, w)] * pn.quad
         + [arr(pn.sums, pn.top + SUB, w), arr(SUB, w)],
         in_specs=[hbm] * 5,
         out_specs=[vm] * (pn.quad + 2),
@@ -247,23 +234,23 @@
             pltpu.VMEM(flag.shape, jnp.int32),
             pltpu.SMEM(rows.shape, jnp.int32),
             pltpu.VMEM(flag.shape, f32),
-            pltpu.SemaphoreType.DMA((2 + 3 * (pn.groups + 1),)),
+            pltpu.SemaphoreType.DMA((2 + 3 * (pn.groups + PIECES),)),
         ],
         compiler_params=large,
         name="sums",
     )(*inputs)
     near = {k: swap(msgs[k], k) for k in NEAR}
-    g = call(functools.partial(weigh_kernel, pn), arr(pn.gsum, w), wt, acc)
+    g = call(functools.partial(weigh_kernel, pn), arr(pn.sums, w), wt, acc)
     step = 1
     while step < pn.lats:
         g = g + lax.ppermute(g, "lat", [(i, i ^ step) for i in range(pn.lats)])
         step *= 2
     part = call(
-        functools.partial(add_kernel, pn), arr(sum(pn.rrows) + pn.gsum, w),
+        functools.partial(add_kernel, pn), arr(pn.rrows + pn.sums, w),
         msgs[0], near[1], near[2], near[3], g,
     )
     far = swap(part, pn.quad)
-    done = call(functools.partial(final_kernel, pn), arr(sum(pn.grows), w), part, far)
+    done = call(functools.partial(final_kernel, pn), arr(pn.grow1 + pn.sums, w), part, far)
     there = {k: swap(done, k) for k in BACK}
     got = [done, there[1], there[2], there[3]]
     outs = pl.pallas_call(

time: 36.3 us -> 35.4 us (0.975)
  waiting for transfers between devices: 16 us -> 15.3 us
    ppermute x7, waiting for transfers between devices: 13 us -> 12.3 us  [swap(): return lax.ppermute(x, 'lon', [(i, i ^ k) for i in range(pn.lons)])]
where the time goes in v1:
time: 35.4 us; the launch traced here: 35.2 us
  waiting for transfers between devices  15.3 us (43%)
  starting transfers between devices  12.9 us (36%)
  Pallas kernels  6.4 us (18%)
  between operations  0.66 us (2%)
    ppermute x7, waiting for transfers between devices, swap(): return lax.ppermute(x, 'lon', [(i, i ^ k) for i in range(pn.lons)])  12.3 us
    ppermute x7, starting transfers between devices, swap(): return lax.ppermute(x, 'lon', [(i, i ^ k) for i in range(pn.lons)])  11 us
    pallas_call x1, Pallas kernels, fast(): pl.pallas_call(functools.partial(sums_kernel, pn), out_shape=[arr(pn.rrow...  4.45 us
    ppermute x2, waiting for transfers between devices, fast(): g = g + lax.ppermute(g, 'lat', [(i, i ^ step) for i in range(pn.lats)])  3.02 us
    ppermute x2, starting transfers between devices, fast(): g = g + lax.ppermute(g, 'lat', [(i, i ^ step) for i in range(pn.lats)])  1.88 us
    pallas_call x3, Pallas kernels, call(): pl.pallas_call(kernel, out_shape=out, in_specs=[vm] * len(args), out_spec...  1.15 us
    pallas_call x1, Pallas kernels, fast(): pl.pallas_call(functools.partial(place_kernel, pn), out_shape=[arr(pn.nva...  0.8 us
  transfers between devices with their start and end apart: 9, of which 7 were waited for; matrix products, arithmetic and copies ran while one was open for 0% of the time, Pallas kernels for 3%

profile of v1, /device:TPU:0, one launch (start us, length us, event | category | flops | bytes accessed | tf_op | source)
XLA Modules:
  0.0 35.2 jit_solution(175300332481869888)
XLA Ops:
  0.6 4.5 %sums.1 = (f32[297,128]{1,0:T(8,128)S(1)}, f32[297,128]{1,0:T(8,128)S(1)}, f32[297,128]{1,0:T(8,128)S(1)}, f32[297,128]{1,0:T(8,128)S(1)}, f32[17,72,128]{2,1,0:T(8,128)S(1)}, /*index=5*/f32[8,128]{1,0:T(8,128)S(1)}) custom-call(f32[69,45,4,128]{3,2,1,0:T(4,128)} %bitcast.6, f32[45,69,128]{2,1,0:T(8,128)} %bitcast.7, f32[45,69,128]{2,1,0:T(8,128)} %bitcast.8, ...), custom_call_target="tpu_custom_call" | custom-call | tf_op jit(solution)/shard_map/sums/pallas_call | solution.py:224
  5.1 3.1 %collective-permute-start = (f32[297,128]{1,0:T(8,128)S(1)}, f32[297,128]{1,0:T(8,128)S(1)}, u32[]{:S(2)}, u32[]{:S(2)}) collective-permute-start(f32[297,128]{1,0:T(8,128)S(1)} %get-tuple-element.19), channel_id=1, source_target_pairs={{0,1},{1,0},{2,3},{3,2},{4,5},{5,4},{6,7},{7,6},{8,9},{9,8},{10,11... | collective-permute-start | bytes 456200 | tf_op jit(solution)/shard_map/ppermute | solution.py:221
  8.2 1.6 %collective-permute-start.1 = (f32[297,128]{1,0:T(8,128)S(1)}, f32[297,128]{1,0:T(8,128)S(1)}, u32[]{:S(2)}, u32[]{:S(2)}) collective-permute-start(f32[297,128]{1,0:T(8,128)S(1)} %get-tuple-element.20), channel_id=1, source_target_pairs={{0,2},{1,3},{2,0},{3,1},{4,6},{5,7},{6,4},{7,5},{8,10},{9,11},{10,... | collective-permute-start | bytes 456200 | tf_op jit(solution)/shard_map/ppermute | solution.py:221
  9.7 0.0 collective-permute-start.2
  9.7 1.1 %shard_map.100 = f32[17,128]{1,0:T(8,128)S(1)} custom-call(f32[8,128]{1,0:T(8,128)S(1)} %get-tuple-element.22.wt, f32[17,72,128]{2,1,0:T(8,128)S(1)} %get-tuple-element.23.acc), custom_call_target="tpu_custom_call" | custom-call | tf_op jit(solution)/shard_map/pallas_call | solution.py:212
  10.8 0.0 collective-permute-start.3
  10.8 1.2 %collective-permute-done.3 = f32[17,128]{1,0:T(8,128)S(1)} collective-permute-done((f32[17,128]{1,0:T(8,128)S(1)}, f32[17,128]{1,0:T(8,128)S(1)}, u32[]{:S(2)}, u32[]{:S(2)}) %collective-permute-start.3) | collective-permute-done | bytes 8736 | tf_op jit(solution)/shard_map/ppermute | solution.py:246
  12.0 1.9 %collective-permute-start.4 = (f32[17,128]{1,0:T(8,128)S(1)}, f32[17,128]{1,0:T(8,128)S(1)}, u32[]{:S(2)}, u32[]{:S(2)}) collective-permute-start(f32[17,128]{1,0:T(8,128)S(1)} %add.6), channel_id=1, source_target_pairs={{0,16},{8,24},{16,0},{24,8},{1,17},{9,25},{17,1},{25,9},{2,18},{10... | collective-permute-start | bytes 26120 | tf_op jit(solution)/shard_map/ppermute | solution.py:246
  13.9 1.8 %collective-permute-done.4 = f32[17,128]{1,0:T(8,128)S(1)} collective-permute-done((f32[17,128]{1,0:T(8,128)S(1)}, f32[17,128]{1,0:T(8,128)S(1)}, u32[]{:S(2)}, u32[]{:S(2)}) %collective-permute-start.4) | collective-permute-done | bytes 8736 | tf_op jit(solution)/shard_map/ppermute | solution.py:246
  15.7 0.0 collective-permute-done.r1
  15.7 0.0 collective-permute-done.1.r2
  15.7 1.1 %collective-permute-done.2.r3 = f32[297,128]{1,0:T(8,128)S(1)} collective-permute-done((f32[297,128]{1,0:T(8,128)S(1)}, f32[297,128]{1,0:T(8,128)S(1)}, u32[]{:S(2)}, u32[]{:S(2)}) %collective-permute-start.2) | collective-permute-done | bytes 152096 | tf_op jit(solution)/shard_map/ppermute | solution.py:221
  16.8 2.8 %collective-permute-start.5 = (f32[314,128]{1,0:T(8,128)S(1)}, f32[314,128]{1,0:T(8,128)S(1)}, u32[]{:S(2)}, u32[]{:S(2)}) collective-permute-start(f32[314,128]{1,0:T(8,128)S(1)} %shard_map.101.own), channel_id=1, source_target_pairs={{0,4},{1,5},{2,6},{3,7},{4,0},{5,1},{6,2},{7,3},{8,12},{9,13},{10,... | collective-permute-start | bytes 482312 | tf_op jit(solution)/shard_map/ppermute | solution.py:221
  19.6 7.0 %collective-permute-done.5.far = f32[314,128]{1,0:T(8,128)S(1)} collective-permute-done((f32[314,128]{1,0:T(8,128)S(1)}, f32[314,128]{1,0:T(8,128)S(1)}, u32[]{:S(2)}, u32[]{:S(2)}) %collective-permute-start.5) | collective-permute-done | bytes 160800 | tf_op jit(solution)/shard_map/ppermute | solution.py:221
  26.6 1.4 %collective-permute-start.8 = (f32[224,128]{1,0:T(8,128)S(1)}, f32[224,128]{1,0:T(8,128)S(1)}, u32[]{:S(2)}, u32[]{:S(2)}) collective-permute-start(f32[224,128]{1,0:T(8,128)S(1)} %shard_map.102.refs_0_), channel_id=1, source_target_pairs={{0,3},{1,2},{2,1},{3,0},{4,7},{5,6},{6,5},{7,4},{8,11},{9,10},{10,... | collective-permute-start | bytes 344072 | tf_op jit(solution)/shard_map/ppermute | solution.py:221
  28.0 1.4 %collective-permute-start.7 = (f32[224,128]{1,0:T(8,128)S(1)}, f32[224,128]{1,0:T(8,128)S(1)}, u32[]{:S(2)}, u32[]{:S(2)}) collective-permute-start(f32[224,128]{1,0:T(8,128)S(1)} %shard_map.102.refs_0_), channel_id=1, source_target_pairs={{0,2},{1,3},{2,0},{3,1},{4,6},{5,7},{6,4},{7,5},{8,10},{9,11},{10,... | collective-permute-start | bytes 344072 | tf_op jit(solution)/shard_map/ppermute | solution.py:221
  29.3 0.8 %collective-permute-start.6 = (f32[224,128]{1,0:T(8,128)S(1)}, f32[224,128]{1,0:T(8,128)S(1)}, u32[]{:S(2)}, u32[]{:S(2)}) collective-permute-start(f32[224,128]{1,0:T(8,128)S(1)} %shard_map.102.refs_0_), channel_id=1, source_target_pairs={{0,1},{1,0},{2,3},{3,2},{4,5},{5,4},{6,7},{7,6},{8,9},{9,8},{10,11... | collective-permute-start | bytes 344072 | tf_op jit(solution)/shard_map/ppermute | solution.py:221
  30.2 3.0 %collective-permute-done.8.refs_3_ = f32[224,128]{1,0:T(8,128)S(1)} collective-permute-done((f32[224,128]{1,0:T(8,128)S(1)}, f32[224,128]{1,0:T(8,128)S(1)}, u32[]{:S(2)}, u32[]{:S(2)}) %collective-permute-start.8) | collective-permute-done | bytes 114720 | tf_op jit(solution)/shard_map/ppermute | solution.py:221
  33.2 0.6 %collective-permute-done.7.refs_2_ = f32[224,128]{1,0:T(8,128)S(1)} collective-permute-done((f32[224,128]{1,0:T(8,128)S(1)}, f32[224,128]{1,0:T(8,128)S(1)}, u32[]{:S(2)}, u32[]{:S(2)}) %collective-permute-start.7) | collective-permute-done | bytes 114720 | tf_op jit(solution)/shard_map/ppermute | solution.py:221
  33.8 0.6 %collective-permute-done.6.refs_1_ = f32[224,128]{1,0:T(8,128)S(1)} collective-permute-done((f32[224,128]{1,0:T(8,128)S(1)}, f32[224,128]{1,0:T(8,128)S(1)}, u32[]{:S(2)}, u32[]{:S(2)}) %collective-permute-start.6) | collective-permute-done | bytes 114720 | tf_op jit(solution)/shard_map/ppermute | solution.py:221
  34.4 0.8 %place.1 = (f32[69,4,128]{2,1,0:T(4,128)}, f32[69,4,128]{2,1,0:T(4,128)}, f32[69,4,128]{2,1,0:T(4,128)}, f32[4,69]{1,0:T(4,128)}, f32[4,69]{1,0:T(4,128)}, /*index=5*/f32[4,69]{1,0:T(4,128)}) custom-call(f32[224,128]{1,0:T(8,128)S(1)} %shard_map.102.refs_0_, f32[224,128]{1,0:T(8,128)S(1)} %collective-permute-done.6.refs_1_, ...), custom_call_target="tpu_custom_call" | custom-call | tf_op jit(solution)/shard_map/place/pallas_call | solution.py:256
  (4 shorter events, 0.1 us)
Async XLA Ops:
  5.1 10.6 %collective-permute-start = (f32[297,128]{1,0:T(8,128)S(1)}, f32[297,128]{1,0:T(8,128)S(1)}, u32[]{:S(2)}, u32[]{:S(2)}) collective-permute-start(f32[297,128]{1,0:T(8,128)S(1)} %get-tuple-element.19), channel_id=1, source_target_pairs={{0,1},{1,0},{2,3},{3,2},{4,5},{5,4},{6,7},{7,6},{8,9},{9,8},{10,11... | collective-permute-start | bytes 456200 | tf_op jit(solution)/shard_map/ppermute | solution.py:221
  8.2 7.6 %collective-permute-start.1 = (f32[297,128]{1,0:T(8,128)S(1)}, f32[297,128]{1,0:T(8,128)S(1)}, u32[]{:S(2)}, u32[]{:S(2)}) collective-permute-start(f32[297,128]{1,0:T(8,128)S(1)} %get-tuple-element.20), channel_id=1, source_target_pairs={{0,2},{1,3},{2,0},{3,1},{4,6},{5,7},{6,4},{7,5},{8,10},{9,11},{10,... | collective-permute-start | bytes 456200 | tf_op jit(solution)/shard_map/ppermute | solution.py:221
  9.7 7.0 %collective-permute-start.2 = (f32[297,128]{1,0:T(8,128)S(1)}, f32[297,128]{1,0:T(8,128)S(1)}, u32[]{:S(2)}, u32[]{:S(2)}) collective-permute-start(f32[297,128]{1,0:T(8,128)S(1)} %get-tuple-element.21), channel_id=1, source_target_pairs={{0,3},{1,2},{2,1},{3,0},{4,7},{5,6},{6,5},{7,4},{8,11},{9,10},{10,... | collective-permute-start | bytes 456200 | tf_op jit(solution)/shard_map/ppermute | solution.py:221
  10.8 1.2 %collective-permute-start.3 = (f32[17,128]{1,0:T(8,128)S(1)}, f32[17,128]{1,0:T(8,128)S(1)}, u32[]{:S(2)}, u32[]{:S(2)}) collective-permute-start(f32[17,128]{1,0:T(8,128)S(1)} %shard_map.100), channel_id=1, source_target_pairs={{0,8},{8,0},{16,24},{24,16},{1,9},{9,1},{17,25},{25,17},{2,10},{10... | collective-permute-start | bytes 26120 | tf_op jit(solution)/shard_map/ppermute | solution.py:246
  12.0 3.7 %collective-permute-start.4 = (f32[17,128]{1,0:T(8,128)S(1)}, f32[17,128]{1,0:T(8,128)S(1)}, u32[]{:S(2)}, u32[]{:S(2)}) collective-permute-start(f32[17,128]{1,0:T(8,128)S(1)} %add.6), channel_id=1, source_target_pairs={{0,16},{8,24},{16,0},{24,8},{1,17},{9,25},{17,1},{25,9},{2,18},{10... | collective-permute-start | bytes 26120 | tf_op jit(solution)/shard_map/ppermute | solution.py:246
  16.8 9.8 %collective-permute-start.5 = (f32[314,128]{1,0:T(8,128)S(1)}, f32[314,128]{1,0:T(8,128)S(1)}, u32[]{:S(2)}, u32[]{:S(2)}) collective-permute-start(f32[314,128]{1,0:T(8,128)S(1)} %shard_map.101.own), channel_id=1, source_target_pairs={{0,4},{1,5},{2,6},{3,7},{4,0},{5,1},{6,2},{7,3},{8,12},{9,13},{10,... | collective-permute-start | bytes 482312 | tf_op jit(solution)/shard_map/ppermute | solution.py:221
  26.6 6.6 %collective-permute-start.8 = (f32[224,128]{1,0:T(8,128)S(1)}, f32[224,128]{1,0:T(8,128)S(1)}, u32[]{:S(2)}, u32[]{:S(2)}) collective-permute-start(f32[224,128]{1,0:T(8,128)S(1)} %shard_map.102.refs_0_), channel_id=1, source_target_pairs={{0,3},{1,2},{2,1},{3,0},{4,7},{5,6},{6,5},{7,4},{8,11},{9,10},{10,... | collective-permute-start | bytes 344072 | tf_op jit(solution)/shard_map/ppermute | solution.py:221
  28.0 5.8 %collective-permute-start.7 = (f32[224,128]{1,0:T(8,128)S(1)}, f32[224,128]{1,0:T(8,128)S(1)}, u32[]{:S(2)}, u32[]{:S(2)}) collective-permute-start(f32[224,128]{1,0:T(8,128)S(1)} %shard_map.102.refs_0_), channel_id=1, source_target_pairs={{0,2},{1,3},{2,0},{3,1},{4,6},{5,7},{6,4},{7,5},{8,10},{9,11},{10,... | collective-permute-start | bytes 344072 | tf_op jit(solution)/shard_map/ppermute | solution.py:221
  29.3 5.1 %collective-permute-start.6 = (f32[224,128]{1,0:T(8,128)S(1)}, f32[224,128]{1,0:T(8,128)S(1)}, u32[]{:S(2)}, u32[]{:S(2)}) collective-permute-start(f32[224,128]{1,0:T(8,128)S(1)} %shard_map.102.refs_0_), channel_id=1, source_target_pairs={{0,1},{1,0},{2,3},{3,2},{4,5},{5,4},{6,7},{7,6},{8,9},{9,8},{10,11... | collective-permute-start | bytes 344072 | tf_op jit(solution)/shard_map/ppermute | solution.py:221

commit v2 on v1

--- a/solution.py
+++ b/solution.py
@@ -15,8 +15,12 @@
 SUB = 8
 UNROLL = 9
 PIECES = 3
-NEAR = (1, 3, 2)
-BACK = (3, 1, 2)
+NEAR = (2, 1, 3)
+BACK = (3, 2, 1)
+
+
+def quarter_of(pn, lon):
+    return lax.rem(lon, pn.quad) ^ (2 * (lon // pn.quad))
 
 
 class Plan:
@@ -73,7 +77,7 @@
     for j in range(pn.sums):
         acc[j, pl.ds(pn.top, SUB), :] = jnp.zeros((SUB, w), jnp.float32)
     me_lat = lax.axis_index("lat")
-    quarter = lax.rem(lax.axis_index("lon"), pn.quad)
+    quarter = quarter_of(pn, lax.axis_index("lon"))
     copies[0].wait()
     first = jnp.int32(0)
     for b in range(pn.lats):
@@ -173,7 +177,7 @@
 
 def place_kernel(pn, *refs):
     lv = pn.leads
-    quarter = lax.rem(lax.axis_index("lon"), pn.quad)
+    quarter = quarter_of(pn, lax.axis_index("lon"))
     got, outs = refs[:pn.quad], refs[pn.quad:]
     flats = [outs[i].reshape(pn.nvar * lv, pn.width) for i in range(3)]
     for k in range(pn.quad):
@@ -249,7 +253,7 @@
         functools.partial(add_kernel, pn), arr(pn.rrows + pn.sums, w),
         msgs[0], near[1], near[2], near[3], g,
     )
-    far = swap(part, pn.quad)
+    far = swap(part, pn.quad ^ 2)
     done = call(functools.partial(final_kernel, pn), arr(pn.grow1 + pn.sums, w), part, far)
     there = {k: swap(done, k) for k in BACK}
     got = [done, there[1], there[2], there[3]]

time: 35.4 us -> 34.1 us (0.963)
  waiting for transfers between devices: 15.3 us -> 12 us
  starting transfers between devices: 12.9 us -> 14.9 us
    ppermute x7, waiting for transfers between devices: 12.3 us -> 8.99 us  [swap(): return lax.ppermute(x, 'lon', [(i, i ^ k) for i in range(pn.lons)])]
    ppermute x7, starting transfers between devices: 11 us -> 13 us  [swap(): return lax.ppermute(x, 'lon', [(i, i ^ k) for i in range(pn.lons)])]
where the time goes in v2:
time: 34.1 us; the launch traced here: 34 us
  starting transfers between devices  14.9 us (44%)
  waiting for transfers between devices  12 us (35%)
  Pallas kernels  6.4 us (19%)
  between operations  0.66 us (2%)
    ppermute x7, starting transfers between devices, swap(): return lax.ppermute(x, 'lon', [(i, i ^ k) for i in range(pn.lons)])  13 us
    ppermute x7, waiting for transfers between devices, swap(): return lax.ppermute(x, 'lon', [(i, i ^ k) for i in range(pn.lons)])  8.99 us
    pallas_call x1, Pallas kernels, fast(): pl.pallas_call(functools.partial(sums_kernel, pn), out_shape=[arr(pn.rrow...  4.45 us
    ppermute x2, waiting for transfers between devices, fast(): g = g + lax.ppermute(g, 'lat', [(i, i ^ step) for i in range(pn.lats)])  3.01 us
    ppermute x2, starting transfers between devices, fast(): g = g + lax.ppermute(g, 'lat', [(i, i ^ step) for i in range(pn.lats)])  1.88 us
    pallas_call x3, Pallas kernels, call(): pl.pallas_call(kernel, out_shape=out, in_specs=[vm] * len(args), out_spec...  1.15 us
    pallas_call x1, Pallas kernels, fast(): pl.pallas_call(functools.partial(place_kernel, pn), out_shape=[arr(pn.nva...  0.8 us
  transfers between devices with their start and end apart: 9, of which 7 were waited for; matrix products, arithmetic and copies ran while one was open for 0% of the time, Pallas kernels for 3%

profile of v2, /device:TPU:0, one launch (start us, length us, event | category | flops | bytes accessed | tf_op | source)
XLA Modules:
  0.0 34.0 jit_solution(10550561376613971500)
XLA Ops:
  0.6 4.5 %sums.1 = (f32[297,128]{1,0:T(8,128)S(1)}, f32[297,128]{1,0:T(8,128)S(1)}, f32[297,128]{1,0:T(8,128)S(1)}, f32[297,128]{1,0:T(8,128)S(1)}, f32[17,72,128]{2,1,0:T(8,128)S(1)}, /*index=5*/f32[8,128]{1,0:T(8,128)S(1)}) custom-call(f32[69,45,4,128]{3,2,1,0:T(4,128)} %bitcast.6, f32[45,69,128]{2,1,0:T(8,128)} %bitcast.7, f32[45,69,128]{2,1,0:T(8,128)} %bitcast.8, ...), custom_call_target="tpu_custom_call" | custom-call | tf_op jit(solution)/shard_map/sums/pallas_call | solution.py:228
  5.1 3.1 %collective-permute-start = (f32[297,128]{1,0:T(8,128)S(1)}, f32[297,128]{1,0:T(8,128)S(1)}, u32[]{:S(2)}, u32[]{:S(2)}) collective-permute-start(f32[297,128]{1,0:T(8,128)S(1)} %get-tuple-element.19), channel_id=1, source_target_pairs={{0,1},{1,0},{2,3},{3,2},{4,5},{5,4},{6,7},{7,6},{8,9},{9,8},{10,11... | collective-permute-start | bytes 456200 | tf_op jit(solution)/shard_map/ppermute | solution.py:225
  8.2 1.6 %collective-permute-start.1 = (f32[297,128]{1,0:T(8,128)S(1)}, f32[297,128]{1,0:T(8,128)S(1)}, u32[]{:S(2)}, u32[]{:S(2)}) collective-permute-start(f32[297,128]{1,0:T(8,128)S(1)} %get-tuple-element.20), channel_id=1, source_target_pairs={{0,2},{1,3},{2,0},{3,1},{4,6},{5,7},{6,4},{7,5},{8,10},{9,11},{10,... | collective-permute-start | bytes 456200 | tf_op jit(solution)/shard_map/ppermute | solution.py:225
  9.7 0.0 collective-permute-start.2
  9.7 1.1 %shard_map.100 = f32[17,128]{1,0:T(8,128)S(1)} custom-call(f32[8,128]{1,0:T(8,128)S(1)} %get-tuple-element.22.wt, f32[17,72,128]{2,1,0:T(8,128)S(1)} %get-tuple-element.23.acc), custom_call_target="tpu_custom_call" | custom-call | tf_op jit(solution)/shard_map/pallas_call | solution.py:216
  10.8 0.0 collective-permute-start.3
  10.8 1.2 %collective-permute-done.3 = f32[17,128]{1,0:T(8,128)S(1)} collective-permute-done((f32[17,128]{1,0:T(8,128)S(1)}, f32[17,128]{1,0:T(8,128)S(1)}, u32[]{:S(2)}, u32[]{:S(2)}) %collective-permute-start.3) | collective-permute-done | bytes 8736 | tf_op jit(solution)/shard_map/ppermute | solution.py:250
  12.0 1.9 %collective-permute-start.4 = (f32[17,128]{1,0:T(8,128)S(1)}, f32[17,128]{1,0:T(8,128)S(1)}, u32[]{:S(2)}, u32[]{:S(2)}) collective-permute-start(f32[17,128]{1,0:T(8,128)S(1)} %add.6), channel_id=1, source_target_pairs={{0,16},{8,24},{16,0},{24,8},{1,17},{9,25},{17,1},{25,9},{2,18},{10... | collective-permute-start | bytes 26120 | tf_op jit(solution)/shard_map/ppermute | solution.py:250
  13.9 1.8 %collective-permute-done.4 = f32[17,128]{1,0:T(8,128)S(1)} collective-permute-done((f32[17,128]{1,0:T(8,128)S(1)}, f32[17,128]{1,0:T(8,128)S(1)}, u32[]{:S(2)}, u32[]{:S(2)}) %collective-permute-start.4) | collective-permute-done | bytes 8736 | tf_op jit(solution)/shard_map/ppermute | solution.py:250
  15.7 0.0 collective-permute-done.r1
  15.7 0.0 collective-permute-done.1.r2
  15.7 1.1 %collective-permute-done.2.r3 = f32[297,128]{1,0:T(8,128)S(1)} collective-permute-done((f32[297,128]{1,0:T(8,128)S(1)}, f32[297,128]{1,0:T(8,128)S(1)}, u32[]{:S(2)}, u32[]{:S(2)}) %collective-permute-start.2) | collective-permute-done | bytes 152096 | tf_op jit(solution)/shard_map/ppermute | solution.py:225
  16.8 3.8 %collective-permute-start.5 = (f32[314,128]{1,0:T(8,128)S(1)}, f32[314,128]{1,0:T(8,128)S(1)}, u32[]{:S(2)}, u32[]{:S(2)}) collective-permute-start(f32[314,128]{1,0:T(8,128)S(1)} %shard_map.101.own), channel_id=1, source_target_pairs={{0,6},{1,7},{2,4},{3,5},{4,2},{5,3},{6,0},{7,1},{8,14},{9,15},{10,... | collective-permute-start | bytes 482312 | tf_op jit(solution)/shard_map/ppermute | solution.py:225
  20.6 3.4 %collective-permute-done.5.far = f32[314,128]{1,0:T(8,128)S(1)} collective-permute-done((f32[314,128]{1,0:T(8,128)S(1)}, f32[314,128]{1,0:T(8,128)S(1)}, u32[]{:S(2)}, u32[]{:S(2)}) %collective-permute-start.5) | collective-permute-done | bytes 160800 | tf_op jit(solution)/shard_map/ppermute | solution.py:225
  24.1 3.9 %collective-permute-start.8 = (f32[224,128]{1,0:T(8,128)S(1)}, f32[224,128]{1,0:T(8,128)S(1)}, u32[]{:S(2)}, u32[]{:S(2)}) collective-permute-start(f32[224,128]{1,0:T(8,128)S(1)} %shard_map.102.refs_0_), channel_id=1, source_target_pairs={{0,3},{1,2},{2,1},{3,0},{4,7},{5,6},{6,5},{7,4},{8,11},{9,10},{10,... | collective-permute-start | bytes 344072 | tf_op jit(solution)/shard_map/ppermute | solution.py:225
  28.0 0.0 collective-permute-start.7
  28.0 0.7 %collective-permute-start.6 = (f32[224,128]{1,0:T(8,128)S(1)}, f32[224,128]{1,0:T(8,128)S(1)}, u32[]{:S(2)}, u32[]{:S(2)}) collective-permute-start(f32[224,128]{1,0:T(8,128)S(1)} %shard_map.102.refs_0_), channel_id=1, source_target_pairs={{0,1},{1,0},{2,3},{3,2},{4,5},{5,4},{6,7},{7,6},{8,9},{9,8},{10,11... | collective-permute-start | bytes 344072 | tf_op jit(solution)/shard_map/ppermute | solution.py:225
  28.7 3.4 %collective-permute-done.8.refs_3_ = f32[224,128]{1,0:T(8,128)S(1)} collective-permute-done((f32[224,128]{1,0:T(8,128)S(1)}, f32[224,128]{1,0:T(8,128)S(1)}, u32[]{:S(2)}, u32[]{:S(2)}) %collective-permute-start.8) | collective-permute-done | bytes 114720 | tf_op jit(solution)/shard_map/ppermute | solution.py:225
  32.0 0.7 %collective-permute-done.7.refs_2_ = f32[224,128]{1,0:T(8,128)S(1)} collective-permute-done((f32[224,128]{1,0:T(8,128)S(1)}, f32[224,128]{1,0:T(8,128)S(1)}, u32[]{:S(2)}, u32[]{:S(2)}) %collective-permute-start.7) | collective-permute-done | bytes 114720 | tf_op jit(solution)/shard_map/ppermute | solution.py:225
  32.8 0.4 %collective-permute-done.6.refs_1_ = f32[224,128]{1,0:T(8,128)S(1)} collective-permute-done((f32[224,128]{1,0:T(8,128)S(1)}, f32[224,128]{1,0:T(8,128)S(1)}, u32[]{:S(2)}, u32[]{:S(2)}) %collective-permute-start.6) | collective-permute-done | bytes 114720 | tf_op jit(solution)/shard_map/ppermute | solution.py:225
  33.2 0.8 %place.1 = (f32[69,4,128]{2,1,0:T(4,128)}, f32[69,4,128]{2,1,0:T(4,128)}, f32[69,4,128]{2,1,0:T(4,128)}, f32[4,69]{1,0:T(4,128)}, f32[4,69]{1,0:T(4,128)}, /*index=5*/f32[4,69]{1,0:T(4,128)}) custom-call(f32[224,128]{1,0:T(8,128)S(1)} %shard_map.102.refs_0_, f32[224,128]{1,0:T(8,128)S(1)} %collective-permute-done.6.refs_1_, ...), custom_call_target="tpu_custom_call" | custom-call | tf_op jit(solution)/shard_map/place/pallas_call | solution.py:260
  (4 shorter events, 0.1 us)
Async XLA Ops:
  5.1 10.6 %collective-permute-start = (f32[297,128]{1,0:T(8,128)S(1)}, f32[297,128]{1,0:T(8,128)S(1)}, u32[]{:S(2)}, u32[]{:S(2)}) collective-permute-start(f32[297,128]{1,0:T(8,128)S(1)} %get-tuple-element.19), channel_id=1, source_target_pairs={{0,1},{1,0},{2,3},{3,2},{4,5},{5,4},{6,7},{7,6},{8,9},{9,8},{10,11... | collective-permute-start | bytes 456200 | tf_op jit(solution)/shard_map/ppermute | solution.py:225
  8.2 7.6 %collective-permute-start.1 = (f32[297,128]{1,0:T(8,128)S(1)}, f32[297,128]{1,0:T(8,128)S(1)}, u32[]{:S(2)}, u32[]{:S(2)}) collective-permute-start(f32[297,128]{1,0:T(8,128)S(1)} %get-tuple-element.20), channel_id=1, source_target_pairs={{0,2},{1,3},{2,0},{3,1},{4,6},{5,7},{6,4},{7,5},{8,10},{9,11},{10,... | collective-permute-start | bytes 456200 | tf_op jit(solution)/shard_map/ppermute | solution.py:225
  9.7 7.0 %collective-permute-start.2 = (f32[297,128]{1,0:T(8,128)S(1)}, f32[297,128]{1,0:T(8,128)S(1)}, u32[]{:S(2)}, u32[]{:S(2)}) collective-permute-start(f32[297,128]{1,0:T(8,128)S(1)} %get-tuple-element.21), channel_id=1, source_target_pairs={{0,3},{1,2},{2,1},{3,0},{4,7},{5,6},{6,5},{7,4},{8,11},{9,10},{10,... | collective-permute-start | bytes 456200 | tf_op jit(solution)/shard_map/ppermute | solution.py:225
  10.8 1.2 %collective-permute-start.3 = (f32[17,128]{1,0:T(8,128)S(1)}, f32[17,128]{1,0:T(8,128)S(1)}, u32[]{:S(2)}, u32[]{:S(2)}) collective-permute-start(f32[17,128]{1,0:T(8,128)S(1)} %shard_map.100), channel_id=1, source_target_pairs={{0,8},{8,0},{16,24},{24,16},{1,9},{9,1},{17,25},{25,17},{2,10},{10... | collective-permute-start | bytes 26120 | tf_op jit(solution)/shard_map/ppermute | solution.py:250
  12.0 3.7 %collective-permute-start.4 = (f32[17,128]{1,0:T(8,128)S(1)}, f32[17,128]{1,0:T(8,128)S(1)}, u32[]{:S(2)}, u32[]{:S(2)}) collective-permute-start(f32[17,128]{1,0:T(8,128)S(1)} %add.6), channel_id=1, source_target_pairs={{0,16},{8,24},{16,0},{24,8},{1,17},{9,25},{17,1},{25,9},{2,18},{10... | collective-permute-start | bytes 26120 | tf_op jit(solution)/shard_map/ppermute | solution.py:250
  16.8 7.2 %collective-permute-start.5 = (f32[314,128]{1,0:T(8,128)S(1)}, f32[314,128]{1,0:T(8,128)S(1)}, u32[]{:S(2)}, u32[]{:S(2)}) collective-permute-start(f32[314,128]{1,0:T(8,128)S(1)} %shard_map.101.own), channel_id=1, source_target_pairs={{0,6},{1,7},{2,4},{3,5},{4,2},{5,3},{6,0},{7,1},{8,14},{9,15},{10,... | collective-permute-start | bytes 482312 | tf_op jit(solution)/shard_map/ppermute | solution.py:225
  24.1 7.9 %collective-permute-start.8 = (f32[224,128]{1,0:T(8,128)S(1)}, f32[224,128]{1,0:T(8,128)S(1)}, u32[]{:S(2)}, u32[]{:S(2)}) collective-permute-start(f32[224,128]{1,0:T(8,128)S(1)} %shard_map.102.refs_0_), channel_id=1, source_target_pairs={{0,3},{1,2},{2,1},{3,0},{4,7},{5,6},{6,5},{7,4},{8,11},{9,10},{10,... | collective-permute-start | bytes 344072 | tf_op jit(solution)/shard_map/ppermute | solution.py:225
  28.0 4.8 %collective-permute-start.7 = (f32[224,128]{1,0:T(8,128)S(1)}, f32[224,128]{1,0:T(8,128)S(1)}, u32[]{:S(2)}, u32[]{:S(2)}) collective-permute-start(f32[224,128]{1,0:T(8,128)S(1)} %shard_map.102.refs_0_), channel_id=1, source_target_pairs={{0,2},{1,3},{2,0},{3,1},{4,6},{5,7},{6,4},{7,5},{8,10},{9,11},{10,... | collective-permute-start | bytes 344072 | tf_op jit(solution)/shard_map/ppermute | solution.py:225
  28.0 5.2 %collective-permute-start.6 = (f32[224,128]{1,0:T(8,128)S(1)}, f32[224,128]{1,0:T(8,128)S(1)}, u32[]{:S(2)}, u32[]{:S(2)}) collective-permute-start(f32[224,128]{1,0:T(8,128)S(1)} %shard_map.102.refs_0_), channel_id=1, source_target_pairs={{0,1},{1,0},{2,3},{3,2},{4,5},{5,4},{6,7},{7,6},{8,9},{9,8},{10,11... | collective-permute-start | bytes 344072 | tf_op jit(solution)/shard_map/ppermute | solution.py:225

commit v3 on v2

--- a/solution.py
+++ b/solution.py
@@ -35,6 +35,8 @@
         self.top = self.groups * SUB
         self.extra = nvar - self.top
         self.sums = 4 * leads + 1
+        self.spare = width - nvar
+        self.packed = self.sums - 2
         self.xrow = self.sums * SUB
         self.rrows = self.chunks * self.xrow + 5 * self.extra
         self.prow = SUB * leads
@@ -49,6 +51,7 @@
             and self.extra > 0
             and self.leads == self.quad
             and self.width == 128
+            and self.spare < self.nvar <= 2 * self.spare
         )
 
 
@@ -132,7 +135,7 @@
 
 
 def weigh_kernel(pn, wt, acc, gout):
-    gout[...] = jnp.zeros((pn.sums, pn.width), jnp.float32)
+    gout[...] = jnp.zeros((pn.packed, pn.width), jnp.float32)
     for j in range(pn.sums):
         d = lax.dot_general(
             wt[...],
@@ -141,12 +144,17 @@
             precision=lax.Precision.HIGHEST,
             preferred_element_type=jnp.float32,
         )
-        gout[pl.ds(j, 1), pl.ds(0, pn.top + SUB)] = d[0:1]
+        if j < pn.packed:
+            gout[pl.ds(j, 1), pl.ds(0, pn.nvar)] = d[0:1, : pn.nvar]
+        else:
+            at = 2 * (j - pn.packed)
+            gout[pl.ds(at, 1), pl.ds(pn.nvar, pn.spare)] = d[0:1, : pn.spare]
+            gout[pl.ds(at + 1, 1), pl.ds(pn.nvar, pn.nvar - pn.spare)] = d[0:1, pn.spare:pn.nvar]
 
 
 def add_kernel(pn, own, r1, r2, r3, g, out):
     out[pl.ds(0, pn.rrows), :] = (own[...] + r1[...]) + (r2[...] + r3[...])
-    out[pl.ds(pn.rrows, pn.sums), :] = g[...]
+    out[pl.ds(pn.rrows, pn.packed), :] = g[...]
 
 
 def metrics(sq, off, pr, sp, tt, n):
@@ -172,7 +180,7 @@
     vals = metrics(*(rows(x + m * pn.extra, pn.extra) for m in range(5)), n)
     for i in range(3):
         out[pl.ds(pn.grow0 + i * pn.extra, pn.extra), :] = vals[i]
-    out[pl.ds(pn.grow1, pn.sums), :] = rows(pn.rrows, pn.sums)
+    out[pl.ds(pn.grow1, pn.packed), :] = rows(pn.rrows, pn.packed)
 
 
 def place_kernel(pn, *refs):
@@ -189,13 +197,17 @@
             flats[i][pl.ds(pn.top * lv + p, pn.extra, stride=lv), :] = got[k][
                 pl.ds(pn.grow0 + i * pn.extra, pn.extra), :
             ]
-    a, b, c, d = (r[pl.ds(pn.grow1, pn.sums), :] for r in got)
+    a, b, c, d = (r[pl.ds(pn.grow1, pn.packed), :] for r in got)
     g = (a + b) + (c + d)
     n = np.float32(pn.lat_total * pn.lon_total)
-    mse, off, skill = metrics(*(g[m * lv:(m + 1) * lv] for m in range(4)), g[4 * lv:4 * lv + 1], n)
-    outs[3][...] = jnp.sqrt(jnp.maximum(mse, FLOOR))[:, : pn.nvar]
-    outs[4][...] = off[:, : pn.nvar]
-    outs[5][...] = skill[:, : pn.nvar]
+    v = pn.nvar
+    late = [jnp.concatenate([g[i:i + 1, v:], g[i + 1:i + 2, v:2 * v - pn.spare]], axis=1) for i in (0, 2)]
+    head = [g[m * lv:(m + 1) * lv, :v] for m in range(3)]
+    spread = jnp.concatenate([g[3 * lv:pn.packed, :v], late[0]], axis=0)
+    mse, off, skill = metrics(*head, spread, late[1], n)
+    outs[3][...] = jnp.sqrt(jnp.maximum(mse, FLOOR))
+    outs[4][...] = off
+    outs[5][...] = skill
 
 
 def fast(pn, pred, truth, norm, flag, rows):
@@ -244,17 +256,17 @@
         name="sums",
     )(*inputs)
     near = {k: swap(msgs[k], k) for k in NEAR}
-    g = call(functools.partial(weigh_kernel, pn), arr(pn.sums, w), wt, acc)
+    g = call(functools.partial(weigh_kernel, pn), arr(pn.packed, w), wt, acc)
     step = 1
     while step < pn.lats:
         g = g + lax.ppermute(g, "lat", [(i, i ^ step) for i in range(pn.lats)])
         step *= 2
     part = call(
-        functools.partial(add_kernel, pn), arr(pn.rrows + pn.sums, w),
+        functools.partial(add_kernel, pn), arr(pn.rrows + pn.packed, w),
         msgs[0], near[1], near[2], near[3], g,
     )
     far = swap(part, pn.quad ^ 2)
-    done = call(functools.partial(final_kernel, pn), arr(pn.grow1 + pn.sums, w), part, far)
+    done = call(functools.partial(final_kernel, pn), arr(pn.grow1 + pn.packed, w), part, far)
     there = {k: swap(done, k) for k in BACK}
     got = [done, there[1], there[2], there[3]]
     outs = pl.pallas_call(

time: 34.1 us -> 33.9 us (level)
  no operation moved by 1% of the time
where the time goes in v3:
time: 33.9 us; the launch traced here: 33.8 us
  starting transfers between devices  14.8 us (44%)
  waiting for transfers between devices  11.8 us (35%)
  Pallas kernels  6.46 us (19%)
  between operations  0.66 us (2%)
    ppermute x7, starting transfers between devices, swap(): return lax.ppermute(x, 'lon', [(i, i ^ k) for i in range(pn.lons)])  12.9 us
    ppermute x7, waiting for transfers between devices, swap(): return lax.ppermute(x, 'lon', [(i, i ^ k) for i in range(pn.lons)])  8.88 us
    pallas_call x1, Pallas kernels, fast(): pl.pallas_call(functools.partial(sums_kernel, pn), out_shape=[arr(pn.rrow...  4.45 us
    ppermute x2, waiting for transfers between devices, fast(): g = g + lax.ppermute(g, 'lat', [(i, i ^ step) for i in range(pn.lats)])  2.97 us
    ppermute x2, starting transfers between devices, fast(): g = g + lax.ppermute(g, 'lat', [(i, i ^ step) for i in range(pn.lats)])  1.88 us
    pallas_call x3, Pallas kernels, call(): pl.pallas_call(kernel, out_shape=out, in_specs=[vm] * len(args), out_spec...  1.22 us
    pallas_call x1, Pallas kernels, fast(): pl.pallas_call(functools.partial(place_kernel, pn), out_shape=[arr(pn.nva...  0.79 us
  transfers between devices with their start and end apart: 9, of which 7 were waited for; matrix products, arithmetic and copies ran while one was open for 0% of the time, Pallas kernels for 3%

profile of v3, /device:TPU:0, one launch (start us, length us, event | category | flops | bytes accessed | tf_op | source)
XLA Modules:
  0.0 33.8 jit_solution(5902418082714491074)
XLA Ops:
  0.6 4.5 %sums.1 = (f32[297,128]{1,0:T(8,128)S(1)}, f32[297,128]{1,0:T(8,128)S(1)}, f32[297,128]{1,0:T(8,128)S(1)}, f32[297,128]{1,0:T(8,128)S(1)}, f32[17,72,128]{2,1,0:T(8,128)S(1)}, /*index=5*/f32[8,128]{1,0:T(8,128)S(1)}) custom-call(f32[69,45,4,128]{3,2,1,0:T(4,128)} %bitcast.6, f32[45,69,128]{2,1,0:T(8,128)} %bitcast.7, f32[45,69,128]{2,1,0:T(8,128)} %bitcast.8, ...), custom_call_target="tpu_custom_call" | custom-call | tf_op jit(solution)/shard_map/sums/pallas_call | solution.py:240
  5.1 3.1 %collective-permute-start = (f32[297,128]{1,0:T(8,128)S(1)}, f32[297,128]{1,0:T(8,128)S(1)}, u32[]{:S(2)}, u32[]{:S(2)}) collective-permute-start(f32[297,128]{1,0:T(8,128)S(1)} %get-tuple-element.19), channel_id=1, source_target_pairs={{0,1},{1,0},{2,3},{3,2},{4,5},{5,4},{6,7},{7,6},{8,9},{9,8},{10,11... | collective-permute-start | bytes 456200 | tf_op jit(solution)/shard_map/ppermute | solution.py:237
  8.2 1.6 %collective-permute-start.1 = (f32[297,128]{1,0:T(8,128)S(1)}, f32[297,128]{1,0:T(8,128)S(1)}, u32[]{:S(2)}, u32[]{:S(2)}) collective-permute-start(f32[297,128]{1,0:T(8,128)S(1)} %get-tuple-element.20), channel_id=1, source_target_pairs={{0,2},{1,3},{2,0},{3,1},{4,6},{5,7},{6,4},{7,5},{8,10},{9,11},{10,... | collective-permute-start | bytes 456200 | tf_op jit(solution)/shard_map/ppermute | solution.py:237
  9.7 0.0 collective-permute-start.2
  9.7 1.1 %shard_map.100 = f32[15,128]{1,0:T(8,128)S(1)} custom-call(f32[8,128]{1,0:T(8,128)S(1)} %get-tuple-element.22.wt, f32[17,72,128]{2,1,0:T(8,128)S(1)} %get-tuple-element.23.acc), custom_call_target="tpu_custom_call" | custom-call | tf_op jit(solution)/shard_map/pallas_call | solution.py:228
  10.9 0.0 collective-permute-start.3
  10.9 1.2 %collective-permute-done.3 = f32[15,128]{1,0:T(8,128)S(1)} collective-permute-done((f32[15,128]{1,0:T(8,128)S(1)}, f32[15,128]{1,0:T(8,128)S(1)}, u32[]{:S(2)}, u32[]{:S(2)}) %collective-permute-start.3) | collective-permute-done | bytes 7712 | tf_op jit(solution)/shard_map/ppermute | solution.py:262
  12.1 1.9 %collective-permute-start.4 = (f32[15,128]{1,0:T(8,128)S(1)}, f32[15,128]{1,0:T(8,128)S(1)}, u32[]{:S(2)}, u32[]{:S(2)}) collective-permute-start(f32[15,128]{1,0:T(8,128)S(1)} %add.6), channel_id=1, source_target_pairs={{0,16},{8,24},{16,0},{24,8},{1,17},{9,25},{17,1},{25,9},{2,18},{10... | collective-permute-start | bytes 23048 | tf_op jit(solution)/shard_map/ppermute | solution.py:262
  13.9 1.8 %collective-permute-done.4 = f32[15,128]{1,0:T(8,128)S(1)} collective-permute-done((f32[15,128]{1,0:T(8,128)S(1)}, f32[15,128]{1,0:T(8,128)S(1)}, u32[]{:S(2)}, u32[]{:S(2)}) %collective-permute-start.4) | collective-permute-done | bytes 7712 | tf_op jit(solution)/shard_map/ppermute | solution.py:262
  15.7 0.0 collective-permute-done.r1
  15.7 0.0 collective-permute-done.1.r2
  15.7 1.0 %collective-permute-done.2.r3 = f32[297,128]{1,0:T(8,128)S(1)} collective-permute-done((f32[297,128]{1,0:T(8,128)S(1)}, f32[297,128]{1,0:T(8,128)S(1)}, u32[]{:S(2)}, u32[]{:S(2)}) %collective-permute-start.2) | collective-permute-done | bytes 152096 | tf_op jit(solution)/shard_map/ppermute | solution.py:237
  16.8 3.8 %collective-permute-start.5 = (f32[312,128]{1,0:T(8,128)S(1)}, f32[312,128]{1,0:T(8,128)S(1)}, u32[]{:S(2)}, u32[]{:S(2)}) collective-permute-start(f32[312,128]{1,0:T(8,128)S(1)} %shard_map.101.own), channel_id=1, source_target_pairs={{0,6},{1,7},{2,4},{3,5},{4,2},{5,3},{6,0},{7,1},{8,14},{9,15},{10,... | collective-permute-start | bytes 479240 | tf_op jit(solution)/shard_map/ppermute | solution.py:237
  20.6 3.3 %collective-permute-done.5.far = f32[312,128]{1,0:T(8,128)S(1)} collective-permute-done((f32[312,128]{1,0:T(8,128)S(1)}, f32[312,128]{1,0:T(8,128)S(1)}, u32[]{:S(2)}, u32[]{:S(2)}) %collective-permute-start.5) | collective-permute-done | bytes 159776 | tf_op jit(solution)/shard_map/ppermute | solution.py:237
  24.0 3.8 %collective-permute-start.8 = (f32[222,128]{1,0:T(8,128)S(1)}, f32[222,128]{1,0:T(8,128)S(1)}, u32[]{:S(2)}, u32[]{:S(2)}) collective-permute-start(f32[222,128]{1,0:T(8,128)S(1)} %shard_map.102.refs_0_), channel_id=1, source_target_pairs={{0,3},{1,2},{2,1},{3,0},{4,7},{5,6},{6,5},{7,4},{8,11},{9,10},{10,... | collective-permute-start | bytes 341000 | tf_op jit(solution)/shard_map/ppermute | solution.py:237
  27.8 0.0 collective-permute-start.7
  27.8 0.7 %collective-permute-start.6 = (f32[222,128]{1,0:T(8,128)S(1)}, f32[222,128]{1,0:T(8,128)S(1)}, u32[]{:S(2)}, u32[]{:S(2)}) collective-permute-start(f32[222,128]{1,0:T(8,128)S(1)} %shard_map.102.refs_0_), channel_id=1, source_target_pairs={{0,1},{1,0},{2,3},{3,2},{4,5},{5,4},{6,7},{7,6},{8,9},{9,8},{10,11... | collective-permute-start | bytes 341000 | tf_op jit(solution)/shard_map/ppermute | solution.py:237
  28.5 3.4 %collective-permute-done.8.refs_3_ = f32[222,128]{1,0:T(8,128)S(1)} collective-permute-done((f32[222,128]{1,0:T(8,128)S(1)}, f32[222,128]{1,0:T(8,128)S(1)}, u32[]{:S(2)}, u32[]{:S(2)}) %collective-permute-start.8) | collective-permute-done | bytes 113696 | tf_op jit(solution)/shard_map/ppermute | solution.py:237
  31.9 0.7 %collective-permute-done.7.refs_2_ = f32[222,128]{1,0:T(8,128)S(1)} collective-permute-done((f32[222,128]{1,0:T(8,128)S(1)}, f32[222,128]{1,0:T(8,128)S(1)}, u32[]{:S(2)}, u32[]{:S(2)}) %collective-permute-start.7) | collective-permute-done | bytes 113696 | tf_op jit(solution)/shard_map/ppermute | solution.py:237
  32.6 0.4 %collective-permute-done.6.refs_1_ = f32[222,128]{1,0:T(8,128)S(1)} collective-permute-done((f32[222,128]{1,0:T(8,128)S(1)}, f32[222,128]{1,0:T(8,128)S(1)}, u32[]{:S(2)}, u32[]{:S(2)}) %collective-permute-start.6) | collective-permute-done | bytes 113696 | tf_op jit(solution)/shard_map/ppermute | solution.py:237
  33.0 0.8 %place.1 = (f32[69,4,128]{2,1,0:T(4,128)}, f32[69,4,128]{2,1,0:T(4,128)}, f32[69,4,128]{2,1,0:T(4,128)}, f32[4,69]{1,0:T(4,128)}, f32[4,69]{1,0:T(4,128)}, /*index=5*/f32[4,69]{1,0:T(4,128)}) custom-call(f32[222,128]{1,0:T(8,128)S(1)} %shard_map.102.refs_0_, f32[222,128]{1,0:T(8,128)S(1)} %collective-permute-done.6.refs_1_, ...), custom_call_target="tpu_custom_call" | custom-call | tf_op jit(solution)/shard_map/place/pallas_call | solution.py:272
  (4 shorter events, 0.1 us)
Async XLA Ops:
  5.1 10.6 %collective-permute-start = (f32[297,128]{1,0:T(8,128)S(1)}, f32[297,128]{1,0:T(8,128)S(1)}, u32[]{:S(2)}, u32[]{:S(2)}) collective-permute-start(f32[297,128]{1,0:T(8,128)S(1)} %get-tuple-element.19), channel_id=1, source_target_pairs={{0,1},{1,0},{2,3},{3,2},{4,5},{5,4},{6,7},{7,6},{8,9},{9,8},{10,11... | collective-permute-start | bytes 456200 | tf_op jit(solution)/shard_map/ppermute | solution.py:237
  8.2 7.6 %collective-permute-start.1 = (f32[297,128]{1,0:T(8,128)S(1)}, f32[297,128]{1,0:T(8,128)S(1)}, u32[]{:S(2)}, u32[]{:S(2)}) collective-permute-start(f32[297,128]{1,0:T(8,128)S(1)} %get-tuple-element.20), channel_id=1, source_target_pairs={{0,2},{1,3},{2,0},{3,1},{4,6},{5,7},{6,4},{7,5},{8,10},{9,11},{10,... | collective-permute-start | bytes 456200 | tf_op jit(solution)/shard_map/ppermute | solution.py:237
  9.7 7.0 %collective-permute-start.2 = (f32[297,128]{1,0:T(8,128)S(1)}, f32[297,128]{1,0:T(8,128)S(1)}, u32[]{:S(2)}, u32[]{:S(2)}) collective-permute-start(f32[297,128]{1,0:T(8,128)S(1)} %get-tuple-element.21), channel_id=1, source_target_pairs={{0,3},{1,2},{2,1},{3,0},{4,7},{5,6},{6,5},{7,4},{8,11},{9,10},{10,... | collective-permute-start | bytes 456200 | tf_op jit(solution)/shard_map/ppermute | solution.py:237
  10.9 1.2 %collective-permute-start.3 = (f32[15,128]{1,0:T(8,128)S(1)}, f32[15,128]{1,0:T(8,128)S(1)}, u32[]{:S(2)}, u32[]{:S(2)}) collective-permute-start(f32[15,128]{1,0:T(8,128)S(1)} %shard_map.100), channel_id=1, source_target_pairs={{0,8},{8,0},{16,24},{24,16},{1,9},{9,1},{17,25},{25,17},{2,10},{10... | collective-permute-start | bytes 23048 | tf_op jit(solution)/shard_map/ppermute | solution.py:262
  12.1 3.7 %collective-permute-start.4 = (f32[15,128]{1,0:T(8,128)S(1)}, f32[15,128]{1,0:T(8,128)S(1)}, u32[]{:S(2)}, u32[]{:S(2)}) collective-permute-start(f32[15,128]{1,0:T(8,128)S(1)} %add.6), channel_id=1, source_target_pairs={{0,16},{8,24},{16,0},{24,8},{1,17},{9,25},{17,1},{25,9},{2,18},{10... | collective-permute-start | bytes 23048 | tf_op jit(solution)/shard_map/ppermute | solution.py:262
  16.8 7.2 %collective-permute-start.5 = (f32[312,128]{1,0:T(8,128)S(1)}, f32[312,128]{1,0:T(8,128)S(1)}, u32[]{:S(2)}, u32[]{:S(2)}) collective-permute-start(f32[312,128]{1,0:T(8,128)S(1)} %shard_map.101.own), channel_id=1, source_target_pairs={{0,6},{1,7},{2,4},{3,5},{4,2},{5,3},{6,0},{7,1},{8,14},{9,15},{10,... | collective-permute-start | bytes 479240 | tf_op jit(solution)/shard_map/ppermute | solution.py:237
  24.0 7.8 %collective-permute-start.8 = (f32[222,128]{1,0:T(8,128)S(1)}, f32[222,128]{1,0:T(8,128)S(1)}, u32[]{:S(2)}, u32[]{:S(2)}) collective-permute-start(f32[222,128]{1,0:T(8,128)S(1)} %shard_map.102.refs_0_), channel_id=1, source_target_pairs={{0,3},{1,2},{2,1},{3,0},{4,7},{5,6},{6,5},{7,4},{8,11},{9,10},{10,... | collective-permute-start | bytes 341000 | tf_op jit(solution)/shard_map/ppermute | solution.py:237
  27.8 4.8 %collective-permute-start.7 = (f32[222,128]{1,0:T(8,128)S(1)}, f32[222,128]{1,0:T(8,128)S(1)}, u32[]{:S(2)}, u32[]{:S(2)}) collective-permute-start(f32[222,128]{1,0:T(8,128)S(1)} %shard_map.102.refs_0_), channel_id=1, source_target_pairs={{0,2},{1,3},{2,0},{3,1},{4,6},{5,7},{6,4},{7,5},{8,10},{9,11},{10,... | collective-permute-start | bytes 341000 | tf_op jit(solution)/shard_map/ppermute | solution.py:237
  27.8 5.2 %collective-permute-start.6 = (f32[222,128]{1,0:T(8,128)S(1)}, f32[222,128]{1,0:T(8,128)S(1)}, u32[]{:S(2)}, u32[]{:S(2)}) collective-permute-start(f32[222,128]{1,0:T(8,128)S(1)} %shard_map.102.refs_0_), channel_id=1, source_target_pairs={{0,1},{1,0},{2,3},{3,2},{4,5},{5,4},{6,7},{7,6},{8,9},{9,8},{10,11... | collective-permute-start | bytes 341000 | tf_op jit(solution)/shard_map/ppermute | solution.py:237
